TPU v7x, 128 devices: a whole 4x4x4 slice. The times are simulated.
128 devices in a mesh: data: 1, fsdp: 2 (over core), ep: 64 (over z, y, x).
Axes of the slice: x: 4, y: 4, z: 4, core: 2. Of those that a mesh axis runs over, the one named last changes fastest.
Arguments:
- x_in: bfloat16 [128, 384, 2048], P(('data', 'fsdp', 'ep'))
- w_qkv: bfloat16 [2048, 6144], P('fsdp')
- w_out: bfloat16 [2048, 2048], P('fsdp')
- w_gate: bfloat16 [64, 2048, 1408], P('ep', 'fsdp')
- w_up: bfloat16 [64, 2048, 1408], P('ep', 'fsdp')
- w_down: bfloat16 [64, 1408, 2048], P('ep', None, 'fsdp')
- ws_gate: bfloat16 [2048, 2816], P('fsdp')
- ws_up: bfloat16 [2048, 2816], P('fsdp')
- ws_down: bfloat16 [2816, 2048], P(None, 'fsdp')
- expert_ids: int32 [128, 384, 6], P(('data', 'fsdp', 'ep'))
- slot_ids: int32 [128, 384, 6], P(('data', 'fsdp', 'ep'))
- gate_vals: bfloat16 [128, 384, 6], P(('data', 'fsdp', 'ep'))
Outputs:
- output: bfloat16 [128, 384, 2048], P(('data', 'fsdp', 'ep'))
All inputs are finite; a program needn't handle non-finite values.
Results may differ from a plain program's by a relative error of at most 0.00961563.
Values are sent between devices in bfloat16 or wider.
A program may use at most 1 GiB of HBM per device.

v0:
```python
import jax
import jax.numpy as jnp
from jax import lax
from jax.sharding import PartitionSpec as P

HEAD_DIM = 128
ROPE_BASE = 10000.0
EPSILON = 1e-6


def rms_norm(values):
    vals_f32 = values.astype(jnp.float32)
    mean_sq = jnp.mean(vals_f32 * vals_f32, axis=-1, keepdims=True)
    return (vals_f32 * lax.rsqrt(mean_sq + EPSILON)).astype(jnp.bfloat16)


def rotary_embed(heads_in, positions):
    half_dim = HEAD_DIM // 2
    inv_freq = ROPE_BASE ** (-jnp.arange(half_dim, dtype=jnp.float32) * (2.0 / HEAD_DIM))
    angles = positions[:, None] * inv_freq[None, :]
    cos_tab = jnp.cos(angles)[:, None, :]
    sin_tab = jnp.sin(angles)[:, None, :]
    vals_f32 = heads_in.astype(jnp.float32)
    first_half = vals_f32[..., :half_dim]
    second_half = vals_f32[..., half_dim:]
    rotated = jnp.concatenate([first_half * cos_tab - second_half * sin_tab, second_half * cos_tab + first_half * sin_tab], axis=-1)
    return rotated.astype(jnp.bfloat16)


def attention_block(x_in, qkv_weight, out_weight):
    n_batch, seq_len, model_dim = x_in.shape
    n_heads = qkv_weight.shape[1] // (3 * HEAD_DIM)
    normed = rms_norm(x_in)
    qkv_proj = jnp.einsum("bsd,dn->bsn", normed, qkv_weight, preferred_element_type=jnp.float32).astype(jnp.bfloat16)
    qkv_proj = qkv_proj.reshape(n_batch, seq_len, 3, n_heads, HEAD_DIM)
    positions = jnp.arange(seq_len, dtype=jnp.float32)
    query_rot = rotary_embed(qkv_proj[:, :, 0], positions)
    key_rot = rotary_embed(qkv_proj[:, :, 1], positions)
    scores = jnp.einsum("bqhd,bkhd->bhqk", query_rot, key_rot, preferred_element_type=jnp.float32) * (HEAD_DIM ** -0.5)
    causal = jnp.arange(seq_len)[:, None] >= jnp.arange(seq_len)[None, :]
    attn_probs = jax.nn.softmax(jnp.where(causal, scores, -1e30), axis=-1).astype(jnp.bfloat16)
    attn_mixed = jnp.einsum("bhqk,bkhd->bqhd", attn_probs, qkv_proj[:, :, 2], preferred_element_type=jnp.float32).astype(jnp.bfloat16)
    attn_out = jnp.einsum("bsn,nm->bsm", attn_mixed.reshape(n_batch, seq_len, n_heads * HEAD_DIM), out_weight, preferred_element_type=jnp.float32)
    return (x_in.astype(jnp.float32) + attn_out).astype(jnp.bfloat16)


def capacity_for(n_tokens, top_k, n_experts):
    return ((5 * n_tokens * top_k) // (4 * n_experts) + 7) // 8 * 8


def dispatch_rows(normed_rows, expert_ids, slot_ids, n_experts, capacity):
    n_tokens, top_k = expert_ids.shape
    kept_mask = slot_ids >= 0
    target = jnp.where(kept_mask, expert_ids * capacity + slot_ids, n_experts * capacity).reshape(-1)
    source_tok = jnp.arange(n_tokens * top_k, dtype=jnp.int32) // top_k
    row_source = jnp.full((n_experts * capacity,), n_tokens, jnp.int32).at[target].set(source_tok, mode="drop")
    buffer = jnp.take(normed_rows, row_source, axis=0, mode="fill", fill_value=0)
    return buffer.reshape(n_experts, capacity, normed_rows.shape[-1])


def combine_rows(expert_out, expert_ids, slot_ids, gate_vals):
    n_experts, capacity, model_dim = expert_out.shape
    kept_mask = slot_ids >= 0
    source_row = jnp.where(kept_mask, expert_ids * capacity + slot_ids, 0)
    picked = jnp.take(expert_out.reshape(n_experts * capacity, model_dim), source_row, axis=0)
    weight = jnp.where(kept_mask, gate_vals, jnp.zeros_like(gate_vals))
    return jnp.einsum("tk,tkd->td", weight, picked, preferred_element_type=jnp.float32)


def expert_ffn(rows_in, gate_w, up_w, down_w):
    gate_act = jnp.einsum("ecd,edf->ecf", rows_in, gate_w, preferred_element_type=jnp.float32)
    up_act = jnp.einsum("ecd,edf->ecf", rows_in, up_w, preferred_element_type=jnp.float32)
    inner_act = (jax.nn.silu(gate_act) * up_act).astype(jnp.bfloat16)
    return jnp.einsum("ecf,efd->ecd", inner_act, down_w, preferred_element_type=jnp.float32).astype(jnp.bfloat16)


def shared_ffn(normed_rows, gate_w, up_w, down_w):
    gate_act = jnp.dot(normed_rows, gate_w, preferred_element_type=jnp.float32)
    up_act = jnp.dot(normed_rows, up_w, preferred_element_type=jnp.float32)
    inner_act = (jax.nn.silu(gate_act) * up_act).astype(jnp.bfloat16)
    return jnp.dot(inner_act, down_w, preferred_element_type=jnp.float32)


def solution(mesh):
    n_ep = mesh.shape["ep"]
    tok_spec = P(("data", "fsdp", "ep"))
    row_spec = P("fsdp", None)

    def local_step(x_in, w_qkv, w_out, w_gate, w_up, w_down, ws_gate, ws_up, ws_down, expert_ids, slot_ids, gate_vals):
        qkv_full = lax.all_gather(w_qkv, "fsdp", axis=0, tiled=True)
        out_full = lax.all_gather(w_out, "fsdp", axis=0, tiled=True)
        gate_full = lax.all_gather(w_gate, "fsdp", axis=1, tiled=True)
        up_full = lax.all_gather(w_up, "fsdp", axis=1, tiled=True)
        down_full = lax.all_gather(w_down, "fsdp", axis=2, tiled=True)
        sgate_full = lax.all_gather(ws_gate, "fsdp", axis=0, tiled=True)
        sup_full = lax.all_gather(ws_up, "fsdp", axis=0, tiled=True)
        sdown_full = lax.all_gather(ws_down, "fsdp", axis=1, tiled=True)
        n_batch, seq_len, model_dim = x_in.shape
        n_tokens = n_batch * seq_len
        top_k = expert_ids.shape[-1]
        n_experts = w_gate.shape[0] * n_ep
        capacity = capacity_for(n_tokens, top_k, n_experts)
        hidden = attention_block(x_in, qkv_full, out_full).reshape(n_tokens, model_dim)
        normed = rms_norm(hidden)
        ids_flat = expert_ids.reshape(n_tokens, top_k)
        slots_flat = slot_ids.reshape(n_tokens, top_k)
        buffer = dispatch_rows(normed, ids_flat, slots_flat, n_experts, capacity)
        received = lax.all_to_all(buffer, "ep", 0, 1, tiled=True)
        expert_out = expert_ffn(received, gate_full, up_full, down_full)
        returned = lax.all_to_all(expert_out, "ep", 1, 0, tiled=True)
        routed = combine_rows(returned, ids_flat, slots_flat, gate_vals.reshape(n_tokens, top_k))
        shared_out = shared_ffn(normed, sgate_full, sup_full, sdown_full)
        summed = hidden.astype(jnp.float32) + shared_out + routed
        return summed.astype(jnp.bfloat16).reshape(n_batch, seq_len, model_dim)

    return jax.shard_map(local_step, mesh=mesh, in_specs=(tok_spec, row_spec, row_spec, P("ep", "fsdp", None), P("ep", "fsdp", None), P("ep", None, "fsdp"), row_spec, row_spec, P(None, "fsdp"), tok_spec, tok_spec, tok_spec), out_specs=tok_spec, check_vma=False)
```

profile of v0, /device:TPU:97, one launch (start us, length us, event | category | flops | bytes accessed | tf_op | source)
XLA Modules:
  0.0 946.1 jit_solution(16266248233507254580)
XLA Ops:
  11.0 9.0 scatter_custom_fusion
  21.9 32.0 %all-gather.9.cloned.1.call-done = bf16[2048,6144]{1,0:T(8,128)(2,1)} async-done(((bf16[1024,6144]{1,0:T(8,128)(2,1)}), bf16[2048,6144]{1,0:T(8,128)(2,1)}) %all-gather.9.cloned.1.call-update) | async-done | bytes 25165840 | tf_op jit(solution)/shard_map/all_gather | solution.py:90
  53.9 15.0 %fusion.25 = bf16[48,8,48,128]{3,1,2,0:T(8,128)(2,1)S(1)} fusion(bf16[2048,6144]{1,0:T(8,128)(2,1)} %all-gather.9.cloned.1.call-done, bf16[1,384,2048]{2,1,0:T(8,128)(2,1)S(1)} %copy-done, f32[384]{0:T(512)S(1)} %add_rsqrt_fusion.1), kind=kOutput, calls=%fused_computation.46 | convolution fusion | flops 9668395008 | bytes 31458816 | tf_op jit(solution)/shard_map/bsd,dn->bsn/dot_general | solution.py:34
  68.9 1.3 copy.60
  70.2 2.0 fusion.59
  72.2 2.9 copy.57
  75.0 0.8 fusion.40
  75.8 2.3 fusion.29
  78.1 1.9 fusion.33
  80.0 5.4 fusion.60
  85.5 5.1 fusion.26
  90.6 7.2 fusion.19
  97.9 1.1 copy-done.3
  99.3 15.9 %gather_fusion = bf16[3072,2048]{1,0:T(8,128)(2,1)} fusion(bf16[384,2048]{1,0:T(8,128)(2,1)S(1)} %fusion.20, s32[3072]{0:T(1024)S(1)} %fusion.49), kind=kCustom, calls=%fused_computation | custom fusion | bytes 25178112 | tf_op jit(solution)/shard_map/jit(_take)/gather | solution.py:57
  115.2 10.6 %broadcast_select_fusion = bf16[64,48,2048]{2,1,0:T(8,128)(2,1)} fusion(bf16[64,48,2048]{2,1,0:T(8,128)(2,1)} %bitcast.99, pred[64,48]{1,0:T(8,128)(4,1)S(1)} %copy-done.10), kind=kLoop, calls=%fused_computation.9 | loop fusion | flops 6291456 | bytes 25168896 | tf_op jit(solution)/shard_map/jit(_take)/select_n | solution.py:57
  125.8 10.0 %all-to-all-start = ((bf16[64,48,2048]{2,1,0:T(8,128)(2,1)}), bf16[64,48,2048]{2,1,0:T(8,128)(2,1)}, u32[]{:S(2)}, u32[]{:S(2)}) async-start(bf16[64,48,2048]{2,1,0:T(8,128)(2,1)} %broadcast_select_fusion), calls=%async_computation | async-start | bytes 25165824 | tf_op jit(solution)/shard_map/all_to_all | solution.py:108
  137.1 180.9 %all-to-all-done = bf16[64,48,2048]{2,1,0:T(8,128)(2,1)} async-done(((bf16[64,48,2048]{2,1,0:T(8,128)(2,1)}), bf16[64,48,2048]{2,1,0:T(8,128)(2,1)}, u32[]{:S(2)}, u32[]{:S(2)}) %all-to-all-start) | async-done | bytes 12582944 | tf_op jit(solution)/shard_map/all_to_all | solution.py:108
  318.1 25.8 %fusion.9 = f32[3072,1408]{1,0:T(8,128)} fusion(bf16[3072,2048]{1,0:T(8,128)(2,1)} %bitcast.20, bf16[1,2048,1408]{2,1,0:T(8,128)(2,1)} %all-gather.19.cloned.1.call-done), kind=kOutput, calls=%fused_computation.19 | convolution fusion | flops 17716740096 | bytes 35651584 | tf_op jit(solution)/shard_map/ecd,edf->ecf/dot_general | solution.py:71
  343.8 27.8 %multiply_convert_fusion.clone.4 = bf16[3072,1408]{1,0:T(8,128)(2,1)} fusion(f32[3072,1408]{1,0:T(8,128)} %fusion.9, bf16[3072,2048]{1,0:T(8,128)(2,1)} %bitcast.20, bf16[1,2048,1408]{2,1,0:T(8,128)(2,1)} %all-gather.21.cloned.1.call-done), kind=kOutput, calls=%fused_computation.4.clone.clone.clone.1 | convolution fusion | flops 17742692352 | bytes 44302336 | tf_op jit(solution)/shard_map/ecd,edf->ecf/dot_general | solution.py:72
  371.6 23.5 %convert_bitcast_fusion = bf16[1,3072,2048]{2,1,0:T(8,128)(2,1)S(1)} fusion(bf16[1,1408,2048]{2,1,0:T(8,128)(2,1)} %all-gather.23.cloned.1.call-done, bf16[3072,1408]{1,0:T(8,128)(2,1)} %multiply_convert_fusion.clone.4), kind=kOutput, calls=%fused_computation.8 | convolution fusion | flops 17723031552 | bytes 27000832 | tf_op jit(solution)/shard_map/ecf,efd->ecd/dot_general | solution.py:74
  395.1 83.6 %copy.98 = bf16[1,3072,2048]{2,0,1:T(2,128)(2,1)} copy(bf16[1,3072,2048]{2,1,0:T(8,128)(2,1)S(1)} %convert_bitcast_fusion) | data formatting | bytes 25165824 | tf_op jit(solution)/shard_map/convert_element_type | solution.py:74
  479.3 75.5 %reduce.7 = bf16[3072,2048]{1,0:T(8,128)(2,1)} reduce(bf16[3072,1,2048]{2,1,0:T(2,128)(2,1)} %bitcast.97, bf16[]{:T(256)} %broadcast.247), dimensions={1}, to_apply=%bitcast.95.reduce_sub_computation | reduce | bytes 25165826
  554.8 24.8 %reshape.386 = bf16[64,2,49152]{2,1,0:T(2,128)(2,1)} reshape(bf16[3072,2048]{1,0:T(8,128)(2,1)} %reduce.7) | data formatting | bytes 25165824
  579.5 34.4 %all-to-all-start.1 = ((bf16[64,2,49152]{2,1,0:T(2,128)(2,1)}), bf16[64,2,49152]{2,1,0:T(2,128)(2,1)}, u32[]{:S(2)}, u32[]{:S(2)}) async-start(bf16[64,2,49152]{2,1,0:T(2,128)(2,1)} %reshape.386), calls=%async_computation.1 | async-start | bytes 25165824 | tf_op jit(solution)/shard_map/all_to_all | solution.py:110
  615.6 9.6 %fusion.63 = f32[384,2816]{1,0:T(8,128)} fusion(bf16[2048,2816]{1,0:T(8,128)(2,1)} %all-gather.13.cloned.1.call-done, bf16[384,2048]{1,0:T(8,128)(2,1)S(1)} %copy-done.4, f32[384]{0:T(512)S(1)} %copy-done.12), kind=kOutput, calls=%fused_computation.105 | convolution fusion | flops 4431544320 | bytes 17434112 | tf_op jit(solution)/shard_map/dot_general | solution.py:78
  625.2 183.9 %all-to-all-done.1 = bf16[64,2,49152]{2,1,0:T(2,128)(2,1)} async-done(((bf16[64,2,49152]{2,1,0:T(2,128)(2,1)}), bf16[64,2,49152]{2,1,0:T(2,128)(2,1)}, u32[]{:S(2)}, u32[]{:S(2)}) %all-to-all-start.1) | async-done | bytes 12582944 | tf_op jit(solution)/shard_map/all_to_all | solution.py:110
  809.1 41.8 %reshape.387 = bf16[3072,1,2048]{2,1,0:T(2,128)(2,1)} reshape(bf16[64,2,49152]{2,1,0:T(2,128)(2,1)} %all-to-all-done.1) | data formatting | bytes 25165824
  850.9 18.7 %copy.97 = bf16[1,3072,2048]{2,1,0:T(8,128)(2,1)} copy(bf16[1,3072,2048]{2,0,1:T(2,128)(2,1)} %bitcast.98) | data formatting | bytes 25165824
  869.7 24.5 %gather_fusion.1 = bf16[2304,2048]{1,0:T(8,128)(2,1)} fusion(bf16[3072,2048]{1,0:T(8,128)(2,1)} %bitcast.96, s32[3072]{0:T(1024)S(1)} %pad_clamp_fusion), kind=kCustom, calls=%fused_computation.1 | custom fusion | bytes 18883584 | tf_op jit(solution)/shard_map/jit(_take)/gather | solution.py:65
  894.2 15.6 %reshape.364 = bf16[384,6,2048]{2,1,0:T(8,128)(2,1)} reshape(bf16[2304,2048]{1,0:T(8,128)(2,1)} %gather_fusion.1) | data formatting | bytes 18874368 | tf_op jit(solution)/shard_map/jit(_take)/gather | solution.py:65
  909.8 8.0 fusion.1
  917.9 20.9 %fusion.23 = bf16[1,384,2048]{2,1,0:T(8,128)(2,1)} fusion(f32[384,1,2048]{2,1,0:T(1,128)} %fusion.1, bf16[2816,2048]{1,0:T(8,128)(2,1)} %all-gather.17.cloned.1.call-done, bf16[384,2048]{1,0:T(8,128)(2,1)S(1)} %copy-done.4, bf16[2048,2816]{1,0:T(8,128)(2,1)} %all-gather.15.cloned.1.call-done, f32[384,2816]{1,0:T(8,128)} %fusion.63, f32[384]{0:T(512)S(1)} %copy-done.12), kind=kOutput, calls=%fused_computation.44 | convolution fusion | flops 8870363136 | bytes 33687040 | tf_op jit(solution)/shard_map/dot_general | solution.py:81
  (74 shorter events, 10.0 us)
Async XLA Ops:
  6.5 47.4 %all-gather.9.cloned.1.call-start = ((), (), s32[]{:S(2)}) async-start(), calls=%async_computation.2 | async-start | bytes 37748736 | tf_op jit(solution)/shard_map/all_gather | solution.py:90
  7.3 83.3 %all-gather.11.cloned.1.call-start = ((), (), s32[]{:S(2)}) async-start(), calls=%async_computation.3 | async-start | bytes 12582912 | tf_op jit(solution)/shard_map/all_gather | solution.py:91
  8.0 129.1 %all-gather.19.cloned.1.call-start = ((), (), s32[]{:S(2)}) async-start(), calls=%async_computation.7 | async-start | bytes 8650752 | tf_op jit(solution)/shard_map/all_gather | solution.py:92
  8.7 1.9 copy-start.6
  8.8 1.9 copy-start.8
  8.8 11.3 %copy-start = (bf16[1,384,2048]{2,1,0:T(8,128)(2,1)S(1)}, bf16[1,384,2048]{2,1,0:T(8,128)(2,1)}, u32[]{:S(2)}) copy-start(bf16[1,384,2048]{2,1,0:T(8,128)(2,1)} %param.12) | copy-start | bytes 4718596
  8.8 335.0 %all-gather.21.cloned.1.call-start = ((), (), s32[]{:S(2)}) async-start(), calls=%async_computation.8 | async-start | bytes 8650752 | tf_op jit(solution)/shard_map/all_gather | solution.py:93
  9.4 362.2 %all-gather.23.cloned.1.call-start = ((), (), s32[]{:S(2)}) async-start(), calls=%async_computation.9 | async-start | bytes 8650752 | tf_op jit(solution)/shard_map/all_gather | solution.py:94
  78.1 1.9 copy-start.5
  80.0 5.4 copy-start.2
  85.5 5.2 copy-start.1
  97.8 1.1 copy-start.3
  97.9 1.1 copy-start.11
  99.3 15.9 %copy-start.10 = (pred[64,48]{1,0:T(8,128)(4,1)S(1)}, pred[64,48]{1,0:T(8,128)(4,1)}, u32[]{:S(2)}) copy-start(pred[64,48]{1,0:T(8,128)(4,1)} %broadcast_in_dim.57) | copy-start | bytes 9220
  125.8 192.2 %all-to-all-start = ((bf16[64,48,2048]{2,1,0:T(8,128)(2,1)}), bf16[64,48,2048]{2,1,0:T(8,128)(2,1)}, u32[]{:S(2)}, u32[]{:S(2)}) async-start(bf16[64,48,2048]{2,1,0:T(8,128)(2,1)} %broadcast_select_fusion), calls=%async_computation | async-start | bytes 25165824 | tf_op jit(solution)/shard_map/all_to_all | solution.py:108
  135.8 479.8 %all-gather.13.cloned.1.call-start = ((), (), s32[]{:S(2)}) async-start(), calls=%async_computation.4 | async-start | bytes 17301504 | tf_op jit(solution)/shard_map/all_gather | solution.py:95
  136.4 781.5 %all-gather.15.cloned.1.call-start = ((), (), s32[]{:S(2)}) async-start(), calls=%async_computation.5 | async-start | bytes 17301504 | tf_op jit(solution)/shard_map/all_gather | solution.py:96
  579.5 229.6 %all-to-all-start.1 = ((bf16[64,2,49152]{2,1,0:T(2,128)(2,1)}), bf16[64,2,49152]{2,1,0:T(2,128)(2,1)}, u32[]{:S(2)}, u32[]{:S(2)}) async-start(bf16[64,2,49152]{2,1,0:T(2,128)(2,1)} %reshape.386), calls=%async_computation.1 | async-start | bytes 25165824 | tf_op jit(solution)/shard_map/all_to_all | solution.py:110
  614.0 0.8 copy-start.7
  614.0 0.8 copy-start.9
  614.0 1.1 copy-start.13
  614.0 1.6 copy-start.4
  614.0 1.6 copy-start.12
  614.0 303.9 %all-gather.17.cloned.1.call-start = ((), (), s32[]{:S(2)}) async-start(), calls=%async_computation.6 | async-start | bytes 17301504 | tf_op jit(solution)/shard_map/all_gather | solution.py:97
Sparse Core Ops, SparseCore 0:
  9.0 44.8 all-gather.8
  55.6 24.8 all-gather.10
  82.1 20.5 all-gather.18
  104.2 20.5 all-gather.20
  126.4 20.5 all-gather.22
  148.5 28.6 all-gather.12
  178.9 28.6 all-gather.14
  616.5 28.5 all-gather.16
where the time goes:
time: 958 us; the launch traced here: 946 us
  waiting for transfers between devices  402 us (42%)
  local copies, waits for them, and re-layouts  243 us (25%)
  matrix products  145 us (15%)
  other arithmetic  96.8 us (10%)
  starting transfers between devices  44.7 us (5%)
  between operations  14.3 us (1%)
    all_to_all x1, waiting for transfers between devices, local_step(): returned = lax.all_to_all(expert_out, 'ep', 1, 0, tiled=True)  184 us
    all_to_all x1, waiting for transfers between devices, local_step(): received = lax.all_to_all(buffer, 'ep', 0, 1, tiled=True)  181 us
    unnamed x34, local copies, waits for them, and re-layouts  91.2 us
    convert_element_type x1, local copies, waits for them, and re-layouts, expert_ffn(): jnp.einsum('ecf,efd->ecd', inner_act, down_w, preferred_element_type=jnp....  83.6 us
    unnamed x1, other arithmetic  75.5 us
    gather x2, local copies, waits for them, and re-layouts, combine_rows(): jnp.take(expert_out.reshape(n_experts * capacity, model_dim), source_row,...  40.1 us
    all_to_all x1, starting transfers between devices, local_step(): returned = lax.all_to_all(expert_out, 'ep', 1, 0, tiled=True)  34.4 us
    all_gather x1, waiting for transfers between devices, local_step(): qkv_full = lax.all_gather(w_qkv, 'fsdp', axis=0, tiled=True)  32 us
  transfers between devices with their start and end apart: 10, of which 3 were waited for; matrix products, arithmetic and copies ran while one was open for 49% of the time, Pallas kernels for 0%

commit v1 on v0

v1 whole, which is shorter than its diff:
```python
import jax
import jax.numpy as jnp
from jax import lax
from jax.sharding import PartitionSpec as P

HEAD_DIM = 128
ROPE_BASE = 10000.0
EPSILON = 1e-6


def rms_norm(values):
    vals_f32 = values.astype(jnp.float32)
    mean_sq = jnp.mean(vals_f32 * vals_f32, axis=-1, keepdims=True)
    return (vals_f32 * lax.rsqrt(mean_sq + EPSILON)).astype(jnp.bfloat16)


def rotary_embed(heads_in, positions):
    half_dim = HEAD_DIM // 2
    inv_freq = ROPE_BASE ** (-jnp.arange(half_dim, dtype=jnp.float32) * (2.0 / HEAD_DIM))
    angles = positions[:, None] * inv_freq[None, :]
    cos_tab = jnp.cos(angles)[:, None, :]
    sin_tab = jnp.sin(angles)[:, None, :]
    vals_f32 = heads_in.astype(jnp.float32)
    first_half = vals_f32[..., :half_dim]
    second_half = vals_f32[..., half_dim:]
    rotated = jnp.concatenate([first_half * cos_tab - second_half * sin_tab, second_half * cos_tab + first_half * sin_tab], axis=-1)
    return rotated.astype(jnp.bfloat16)


def dot32(left, right):
    return jnp.dot(left, right, preferred_element_type=jnp.float32)


def split_cols(values, fs):
    half = values.shape[-1] // 2
    own = lax.dynamic_slice_in_dim(values, fs * half, half, axis=values.ndim - 1)
    other = lax.dynamic_slice_in_dim(values, (1 - fs) * half, half, axis=values.ndim - 1)
    return own, other


def paired_dot(own_other, pair):
    return dot32(own_other[0], pair[0]) + dot32(own_other[1], pair[1])


def join_cols(left, pair, fs):
    own, other = dot32(left, pair[0]), dot32(left, pair[1])
    return jnp.where(fs == 0, jnp.concatenate([own, other], axis=1), jnp.concatenate([other, own], axis=1))


def attention_block(x_in, qkv_pair, out_pair, fs):
    n_batch, seq_len, model_dim = x_in.shape
    n_heads = qkv_pair[0].shape[1] // (3 * HEAD_DIM)
    normed = rms_norm(x_in).reshape(n_batch * seq_len, model_dim)
    qkv_proj = paired_dot(split_cols(normed, fs), qkv_pair).astype(jnp.bfloat16)
    qkv_proj = qkv_proj.reshape(n_batch, seq_len, 3, n_heads, HEAD_DIM)
    positions = jnp.arange(seq_len, dtype=jnp.float32)
    query_rot = rotary_embed(qkv_proj[:, :, 0], positions)
    key_rot = rotary_embed(qkv_proj[:, :, 1], positions)
    scores = jnp.einsum("bqhd,bkhd->bhqk", query_rot, key_rot, preferred_element_type=jnp.float32) * (HEAD_DIM ** -0.5)
    causal = jnp.arange(seq_len)[:, None] >= jnp.arange(seq_len)[None, :]
    attn_probs = jax.nn.softmax(jnp.where(causal, scores, -1e30), axis=-1).astype(jnp.bfloat16)
    attn_mixed = jnp.einsum("bhqk,bkhd->bqhd", attn_probs, qkv_proj[:, :, 2], preferred_element_type=jnp.float32).astype(jnp.bfloat16)
    mixed = split_cols(attn_mixed.reshape(n_batch * seq_len, n_heads * HEAD_DIM), fs)
    return (x_in.reshape(n_batch * seq_len, model_dim).astype(jnp.float32) + paired_dot(mixed, out_pair)).astype(jnp.bfloat16)


def capacity_for(n_tokens, top_k, n_experts):
    return ((5 * n_tokens * top_k) // (4 * n_experts) + 7) // 8 * 8


def solution(mesh):
    n_ep = mesh.shape["ep"]
    tok_spec = P(("data", "fsdp", "ep"))
    row_spec = P("fsdp", None)

    def local_step(x_in, w_qkv, w_out, w_gate, w_up, w_down, ws_gate, ws_up, ws_down, expert_ids, slot_ids, gate_vals):
        n_batch, seq_len, model_dim = x_in.shape
        n_tokens = n_batch * seq_len
        top_k = expert_ids.shape[-1]
        n_experts = w_gate.shape[0] * n_ep
        capacity = capacity_for(n_tokens, top_k, n_experts)
        n_rows = n_experts * capacity
        fs = lax.axis_index("fsdp")

        def paired(weight):
            return weight, lax.ppermute(weight, "fsdp", [(0, 1), (1, 0)])

        qkv_pair, out_pair = paired(w_qkv), paired(w_out)
        gate_pair, up_pair, down_pair = paired(w_gate[0]), paired(w_up[0]), paired(w_down[0])
        sgate_pair, sup_pair, sdown_pair = paired(ws_gate), paired(ws_up), paired(ws_down)

        ids_flat = expert_ids.reshape(n_tokens, top_k)
        slots_flat = slot_ids.reshape(n_tokens, top_k)
        row_of = jnp.where(slots_flat >= 0, ids_flat * capacity + slots_flat, -1)
        row_iota = jnp.arange(n_rows, dtype=jnp.int32)
        gates = gate_vals.reshape(n_tokens, top_k)
        picks = sum((row_iota[:, None] == row_of[None, :, k]).astype(jnp.bfloat16) for k in range(top_k))
        spread = sum(jnp.where(row_of[:, k, None] == row_iota[None, :], gates[:, k, None], jnp.bfloat16(0)) for k in range(top_k))

        hidden = attention_block(x_in, qkv_pair, out_pair, fs)
        normed = rms_norm(hidden)
        buffer = dot32(picks, normed).astype(jnp.bfloat16).reshape(n_experts, capacity, model_dim)
        received = lax.all_to_all(buffer, "ep", 0, 0, tiled=True).reshape(n_rows, model_dim)

        halves = split_cols(normed, fs)
        shared_act = (jax.nn.silu(paired_dot(halves, sgate_pair)) * paired_dot(halves, sup_pair)).astype(jnp.bfloat16)
        base = hidden.astype(jnp.float32) + join_cols(shared_act, sdown_pair, fs)

        got = split_cols(received, fs)
        act = (jax.nn.silu(paired_dot(got, gate_pair)) * paired_dot(got, up_pair)).astype(jnp.bfloat16)
        expert_out = join_cols(act, down_pair, fs).astype(jnp.bfloat16).reshape(n_experts, capacity, model_dim)
        returned = lax.all_to_all(expert_out, "ep", 0, 0, tiled=True).reshape(n_rows, model_dim)
        summed = base + dot32(spread, returned)
        return summed.astype(jnp.bfloat16).reshape(n_batch, seq_len, model_dim)

    return jax.shard_map(local_step, mesh=mesh, in_specs=(tok_spec, row_spec, row_spec, P("ep", "fsdp", None), P("ep", "fsdp", None), P("ep", None, "fsdp"), row_spec, row_spec, P(None, "fsdp"), tok_spec, tok_spec, tok_spec), out_specs=tok_spec, check_vma=False)
```

time: 958 us -> 629 us (0.66)
  the two profiles are of different devices: /device:TPU:97 before, /device:TPU:8 now
where the time goes in v1:
time: 629 us; the launch traced here: 619 us
  waiting for transfers between devices  357 us (57%)
  matrix products  191 us (30%)
  starting transfers between devices  39.7 us (6%)
  other arithmetic  22.2 us (4%)
  local copies, waits for them, and re-layouts  8.01 us (1%)
    all_to_all x1, waiting for transfers between devices, local_step(): lax.all_to_all(buffer, 'ep', 0, 0, tiled=True).reshape(n_rows, model_dim)  190 us
    dot_general x18, matrix products, dot32(): return jnp.dot(left, right, preferred_element_type=jnp.float32)  184 us
    all_to_all x1, waiting for transfers between devices, local_step(): lax.all_to_all(expert_out, 'ep', 0, 0, tiled=True)  163 us
    all_to_all x1, starting transfers between devices, local_step(): lax.all_to_all(expert_out, 'ep', 0, 0, tiled=True)  26.3 us
  transfers between devices with their start and end apart: 10, of which 3 were waited for; matrix products, arithmetic and copies ran while one was open for 27% of the time, Pallas kernels for 0%

profile of v1, /device:TPU:8, one launch (start us, length us, event | category | flops | bytes accessed | tf_op | source)
XLA Modules:
  0.0 619.0 jit_solution(2882005622426890590)
XLA Ops:
  2.6 1.8 fusion.32
  5.2 1.7 fusion.33
  6.9 8.0 %fusion.95 = f32[384,6144]{1,0:T(8,128)S(1)} fusion(bf16[1024,6144]{1,0:T(8,128)(2,1)} %param.13, bf16[1,384,2048]{2,1,0:T(8,128)(2,1)S(1)} %fusion.33, s32[]{:T(128)S(6)} %select_n.60), kind=kOutput, calls=%fused_computation.116 | convolution fusion | flops 4831838208 | bytes 22806532 | tf_op jit(solution)/shard_map/dot_general | solution.py:31
  15.0 4.2 collective-permute-done
  19.1 10.3 %fusion.71 = bf16[48,8,48,128]{3,1,2,0:T(8,128)(2,1)S(1)} fusion(f32[384,6144]{1,0:T(8,128)S(1)} %fusion.95, bf16[1024,6144]{1,0:T(8,128)(2,1)} %collective-permute-done, bf16[1,384,2048]{2,1,0:T(8,128)(2,1)S(1)} %fusion.33, s32[]{:T(128)S(6)} %select_n.61), kind=kOutput, calls=%fused_computation.90 | convolution fusion | flops 4836556800 | bytes 27525124 | tf_op jit(solution)/shard_map/dot_general | solution.py:31
  30.6 2.0 fusion.129
  32.6 2.9 copy.19
  36.2 2.3 fusion.75
  38.6 1.9 fusion.77
  40.5 5.3 fusion.130
  45.9 5.1 fusion.72
  51.0 1.9 fusion.98
  52.9 4.5 fusion.26
  59.0 11.7 %convolution_convert_fusion = bf16[3072,2048]{1,0:T(8,128)(2,1)} fusion(bf16[384,2048]{1,0:T(8,128)(2,1)S(1)} %fusion.27, s32[384]{0:T(512)S(1)} %get-tuple-element.6, s32[384]{0:T(512)S(1)} %get-tuple-element.7, s32[384]{0:T(512)S(1)} %get-tuple-element.8, s32[384]{0:T(512)S(1)} %copy-done.15, s32[384]{0:T(512)S(1)} %copy-done.17, s32[384]{0:T(512)S(1)} %get-tuple-element.5), kind=kOutput, calls=%fused_computation.4 | convolution fusion | flops 4866441216 | bytes 14164992 | tf_op jit(solution)/shard_map/dot_general | solution.py:31
  70.6 11.6 %all-to-all-start = ((bf16[64,48,2048]{2,1,0:T(8,128)(2,1)}), bf16[64,48,2048]{2,1,0:T(8,128)(2,1)}, u32[]{:S(2)}, u32[]{:S(2)}) async-start(bf16[64,48,2048]{2,1,0:T(8,128)(2,1)} %bitcast.83), calls=%async_computation | async-start | bytes 25165824 | tf_op jit(solution)/shard_map/all_to_all | solution.py:103
  82.9 189.9 %all-to-all-done = bf16[64,48,2048]{2,1,0:T(8,128)(2,1)} async-done(((bf16[64,48,2048]{2,1,0:T(8,128)(2,1)}), bf16[64,48,2048]{2,1,0:T(8,128)(2,1)}, u32[]{:S(2)}, u32[]{:S(2)}) %all-to-all-start) | async-done | bytes 12582944 | tf_op jit(solution)/shard_map/all_to_all | solution.py:103
  272.8 16.8 %fusion.6 = f32[3072,1408]{1,0:T(8,128)} fusion(bf16[3072,2048]{1,0:T(8,128)(2,1)} %bitcast.19, s32[]{:T(128)S(6)} %select_n.60, bf16[1,1024,1408]{2,1,0:T(8,128)(2,1)} %param.16), kind=kOutput, calls=%fused_computation.13 | convolution fusion | flops 8858370048 | bytes 26476548 | tf_op jit(solution)/shard_map/dot_general | solution.py:31
  289.6 15.4 %fusion.8 = f32[3072,1408]{1,0:T(8,128)} fusion(bf16[3072,2048]{1,0:T(8,128)(2,1)} %bitcast.19, s32[]{:T(128)S(6)} %select_n.60, bf16[1,1024,1408]{2,1,0:T(8,128)(2,1)S(1)} %copy-done.19), kind=kOutput, calls=%fused_computation.15 | convolution fusion | flops 8858370048 | bytes 26476548 | tf_op jit(solution)/shard_map/dot_general | solution.py:31
  305.0 16.3 %fusion.4 = f32[3072,1408]{1,0:T(8,128)} fusion(bf16[1024,1408]{1,0:T(8,128)(2,1)} %collective-permute-done.5, bf16[3072,2048]{1,0:T(8,128)(2,1)} %bitcast.19, s32[]{:T(128)S(6)} %select_n.61), kind=kOutput, calls=%fused_computation.11 | convolution fusion | flops 8858370048 | bytes 26476548 | tf_op jit(solution)/shard_map/dot_general | solution.py:31
  321.3 27.4 %multiply_convert_fusion = bf16[3072,1408]{1,0:T(8,128)(2,1)} fusion(f32[3072,1408]{1,0:T(8,128)} %fusion.6, f32[3072,1408]{1,0:T(8,128)} %fusion.8, f32[3072,1408]{1,0:T(8,128)} %fusion.4, bf16[1024,1408]{1,0:T(8,128)(2,1)} %collective-permute-done.6, bf16[3072,2048]{1,0:T(8,128)(2,1)} %bitcast.19, s32[]{:T(128)S(6)} %select_n.61), kind=kOutput, calls=%fused_computation.3 | convolution fusion | flops 8892973056 | bytes 69730304 | tf_op jit(solution)/shard_map/dot_general | solution.py:31
  348.7 13.4 %fusion.34 = bf16[64,48,1024]{2,1,0:T(8,128)(2,1)S(1)} fusion(bf16[64,48,1408]{2,1,0:T(8,128)(2,1)} %bitcast.94, bf16[1,1408,1024]{2,1,0:T(8,128)(2,1)} %param.17), kind=kOutput, calls=%fused_computation.65 | convolution fusion | flops 8858370048 | bytes 17825792 | tf_op jit(solution)/shard_map/dot_general | solution.py:31
  362.2 11.7 %fusion.133 = bf16[3072,1024]{1,0:T(8,128)(2,1)S(1)} fusion(bf16[3072,1408]{1,0:T(8,128)(2,1)S(1)} %copy-done.20, bf16[1408,1024]{1,0:T(8,128)(2,1)} %collective-permute-done.7), kind=kOutput, calls=%fused_computation.173 | convolution fusion | flops 8858370048 | bytes 17825792 | tf_op jit(solution)/shard_map/dot_general | solution.py:31
  373.9 7.7 %fusion.1 = bf16[64,48,2048]{2,1,0:T(8,128)(2,1)} fusion(bf16[64,48,1024]{2,1,0:T(8,128)(2,1)S(1)} %bitcast.84, bf16[64,48,1024]{2,1,0:T(8,128)(2,1)S(1)} %fusion.34, pred[]{:T(512)S(6)} %eq.172), kind=kLoop, calls=%fused_computation.2 | loop fusion | flops 56623104 | bytes 25165824 | tf_op jit(solution)/shard_map/convert_element_type | solution.py:111
  381.6 26.3 %all-to-all-start.1 = ((bf16[64,48,2048]{2,1,0:T(8,128)(2,1)}), bf16[64,48,2048]{2,1,0:T(8,128)(2,1)}, u32[]{:S(2)}, u32[]{:S(2)}) async-start(bf16[64,48,2048]{2,1,0:T(8,128)(2,1)} %fusion.1), calls=%async_computation.1 | async-start | bytes 25165824 | tf_op jit(solution)/shard_map/all_to_all | solution.py:112
  408.7 7.0 %fusion.105 = f32[384,2816]{1,0:T(8,128)} fusion(bf16[1024,2816]{1,0:T(8,128)(2,1)} %param.19, bf16[384,2048]{1,0:T(8,128)(2,1)S(1)} %fusion.27, s32[]{:T(128)S(6)} %select_n.60), kind=kOutput, calls=%fused_computation.126 | convolution fusion | flops 2214592512 | bytes 10878980 | tf_op jit(solution)/shard_map/dot_general | solution.py:31
  415.7 7.0 %fusion.107 = f32[384,2816]{1,0:T(8,128)} fusion(bf16[1024,2816]{1,0:T(8,128)(2,1)} %param.18, bf16[384,2048]{1,0:T(8,128)(2,1)S(1)} %fusion.27, s32[]{:T(128)S(6)} %select_n.60), kind=kOutput, calls=%fused_computation.128 | convolution fusion | flops 2214592512 | bytes 10878980 | tf_op jit(solution)/shard_map/dot_general | solution.py:31
  422.7 4.5 fusion.103
  427.2 7.6 %multiply_convert_fusion.1 = bf16[384,2816]{1,0:T(8,128)(2,1)S(1)} fusion(f32[384,2816]{1,0:T(8,128)} %fusion.105, f32[384,2816]{1,0:T(8,128)} %fusion.107, f32[384,2816]{1,0:T(8,128)} %fusion.103, bf16[1024,2816]{1,0:T(8,128)(2,1)S(1)} %collective-permute-done.3, bf16[384,2048]{1,0:T(8,128)(2,1)S(1)} %fusion.27, s32[]{:T(128)S(6)} %select_n.61), kind=kOutput, calls=%fused_computation.51 | convolution fusion | flops 2223243264 | bytes 21692420 | tf_op jit(solution)/shard_map/dot_general | solution.py:31
  434.9 2.4 fusion.131
  437.4 3.6 fusion.132
  441.0 162.9 %all-to-all-done.1 = bf16[64,48,2048]{2,1,0:T(8,128)(2,1)} async-done(((bf16[64,48,2048]{2,1,0:T(8,128)(2,1)}), bf16[64,48,2048]{2,1,0:T(8,128)(2,1)}, u32[]{:S(2)}, u32[]{:S(2)}) %all-to-all-start.1) | async-done | bytes 12582944 | tf_op jit(solution)/shard_map/all_to_all | solution.py:112
  604.0 14.6 %fusion.36 = bf16[1,384,2048]{2,1,0:T(8,128)(2,1)} fusion(bf16[3072,2048]{1,0:T(8,128)(2,1)} %bitcast.26, f32[384,1024]{1,0:T(8,128)S(1)} %fusion.131, f32[384,1024]{1,0:T(8,128)} %fusion.132, bf16[384,2048]{1,0:T(8,128)(2,1)S(1)} %copy-done.3, s32[384]{0:T(512)S(1)} %copy-done.10, s32[384]{0:T(512)S(1)} %copy-done.12, s32[384]{0:T(512)S(1)} %copy-done.14, ...), kind=kOutput, calls=%fused_computation.67 | convolution fusion | flops 4865654784 | bytes 18888192 | tf_op jit(solution)/shard_map/dot_general | solution.py:31
  (74 shorter events, 8.3 us)
Async XLA Ops:
  0.0 19.1 %collective-permute-start = (bf16[1024,6144]{1,0:T(8,128)(2,1)}, bf16[1024,6144]{1,0:T(8,128)(2,1)}, u32[]{:S(2)}, u32[]{:S(2)}) collective-permute-start(bf16[1024,6144]{1,0:T(8,128)(2,1)} %param.13), channel_id=1, source_target_pairs={{0,64},{64,0},{1,65},{65,1},{2,66},{66,2},{3,67},{67,3},{4,68},{68... | collective-permute-start | bytes 37748744 | tf_op jit(solution)/shard_map/ppermute | solution.py:86
  0.0 52.9 %collective-permute-start.1 = (bf16[1024,2048]{1,0:T(8,128)(2,1)}, bf16[1024,2048]{1,0:T(8,128)(2,1)}, u32[]{:S(2)}, u32[]{:S(2)}) collective-permute-start(bf16[1024,2048]{1,0:T(8,128)(2,1)} %param.14), channel_id=1, source_target_pairs={{0,64},{64,0},{1,65},{65,1},{2,66},{66,2},{3,67},{67,3},{4,68},{68... | collective-permute-start | bytes 12582920 | tf_op jit(solution)/shard_map/ppermute | solution.py:86
  1.9 57.0 %copy-start.7 = (s32[384]{0:T(512)}, s32[384]{0:T(512)S(1)}, u32[]{:S(2)}) copy-start(s32[384]{0:T(512)S(1)} %get-tuple-element.5) | copy-start | bytes 4612
  1.9 57.0 %copy-start.9 = (s32[384]{0:T(512)}, s32[384]{0:T(512)S(1)}, u32[]{:S(2)}) copy-start(s32[384]{0:T(512)S(1)} %get-tuple-element.6) | copy-start | bytes 4612
  1.9 57.0 %copy-start.11 = (s32[384]{0:T(512)}, s32[384]{0:T(512)S(1)}, u32[]{:S(2)}) copy-start(s32[384]{0:T(512)S(1)} %get-tuple-element.7) | copy-start | bytes 4612
  1.9 57.0 %copy-start.13 = (s32[384]{0:T(512)}, s32[384]{0:T(512)S(1)}, u32[]{:S(2)}) copy-start(s32[384]{0:T(512)S(1)} %get-tuple-element.8) | copy-start | bytes 4612
  38.6 1.9 copy-start.5
  40.5 5.4 copy-start.4
  45.8 5.2 copy-start.1
  51.0 1.9 copy-start
  52.9 6.0 copy-start.15
  52.9 6.0 copy-start.17
  70.6 202.1 %all-to-all-start = ((bf16[64,48,2048]{2,1,0:T(8,128)(2,1)}), bf16[64,48,2048]{2,1,0:T(8,128)(2,1)}, u32[]{:S(2)}, u32[]{:S(2)}) async-start(bf16[64,48,2048]{2,1,0:T(8,128)(2,1)} %bitcast.83), calls=%async_computation | async-start | bytes 25165824 | tf_op jit(solution)/shard_map/all_to_all | solution.py:103
  82.2 222.8 %collective-permute-start.5 = (bf16[1024,1408]{1,0:T(8,128)(2,1)}, bf16[1024,1408]{1,0:T(8,128)(2,1)}, u32[]{:S(2)}, u32[]{:S(2)}) collective-permute-start(bf16[1024,1408]{1,0:T(8,128)(2,1)} %bitcast.91), channel_id=1, source_target_pairs={{0,64},{64,0},{1,65},{65,1},{2,66},{66,2},{3,67},{67,3},{4,68},{68... | collective-permute-start | bytes 8650760 | tf_op jit(solution)/shard_map/ppermute | solution.py:86
  82.3 239.0 %collective-permute-start.6 = (bf16[1024,1408]{1,0:T(8,128)(2,1)}, bf16[1024,1408]{1,0:T(8,128)(2,1)}, u32[]{:S(2)}, u32[]{:S(2)}) collective-permute-start(bf16[1024,1408]{1,0:T(8,128)(2,1)} %bitcast.92), channel_id=1, source_target_pairs={{0,64},{64,0},{1,65},{65,1},{2,66},{66,2},{3,67},{67,3},{4,68},{68... | collective-permute-start | bytes 8650760 | tf_op jit(solution)/shard_map/ppermute | solution.py:86
  82.8 279.3 %collective-permute-start.7 = (bf16[1408,1024]{1,0:T(8,128)(2,1)}, bf16[1408,1024]{1,0:T(8,128)(2,1)}, u32[]{:S(2)}, u32[]{:S(2)}) collective-permute-start(bf16[1408,1024]{1,0:T(8,128)(2,1)} %bitcast.93), channel_id=1, source_target_pairs={{0,64},{64,0},{1,65},{65,1},{2,66},{66,2},{3,67},{67,3},{4,68},{68... | collective-permute-start | bytes 8650760 | tf_op jit(solution)/shard_map/ppermute | solution.py:86
  272.8 16.8 %copy-start.19 = (bf16[1,1024,1408]{2,1,0:T(8,128)(2,1)S(1)}, bf16[1,1024,1408]{2,1,0:T(8,128)(2,1)}, u32[]{:S(2)}) copy-start(bf16[1,1024,1408]{2,1,0:T(8,128)(2,1)} %param.15) | copy-start | bytes 8650756
  348.7 13.5 %copy-start.20 = (bf16[3072,1408]{1,0:T(8,128)(2,1)S(1)}, bf16[3072,1408]{1,0:T(8,128)(2,1)}, u32[]{:S(2)}) copy-start(bf16[3072,1408]{1,0:T(8,128)(2,1)} %multiply_convert_fusion) | copy-start | bytes 25952260
  381.6 27.0 %copy-start.6 = (bf16[1,384,6]{1,2,0:T(8,128)(2,1)S(1)}, bf16[1,384,6]{1,2,0:T(8,128)(2,1)}, u32[]{:S(2)}) copy-start(bf16[1,384,6]{1,2,0:T(8,128)(2,1)} %param.23) | copy-start | bytes 13828
  381.6 222.3 %all-to-all-start.1 = ((bf16[64,48,2048]{2,1,0:T(8,128)(2,1)}), bf16[64,48,2048]{2,1,0:T(8,128)(2,1)}, u32[]{:S(2)}, u32[]{:S(2)}) async-start(bf16[64,48,2048]{2,1,0:T(8,128)(2,1)} %fusion.1), calls=%async_computation.1 | async-start | bytes 25165824 | tf_op jit(solution)/shard_map/all_to_all | solution.py:112
  407.9 14.8 %collective-permute-start.2 = (bf16[1024,2816]{1,0:T(8,128)(2,1)}, bf16[1024,2816]{1,0:T(8,128)(2,1)S(1)}, u32[]{:S(2)}, u32[]{:S(2)}) collective-permute-start(bf16[1024,2816]{1,0:T(8,128)(2,1)} %param.18), channel_id=1, source_target_pairs={{0,64},{64,0},{1,65},{65,1},{2,66},{66,2},{3,67},{67,3},{4,68},{68... | collective-permute-start | bytes 17301512 | tf_op jit(solution)/shard_map/ppermute | solution.py:86
  408.0 19.2 %collective-permute-start.3 = (bf16[1024,2816]{1,0:T(8,128)(2,1)}, bf16[1024,2816]{1,0:T(8,128)(2,1)S(1)}, u32[]{:S(2)}, u32[]{:S(2)}) collective-permute-start(bf16[1024,2816]{1,0:T(8,128)(2,1)} %param.19), channel_id=1, source_target_pairs={{0,64},{64,0},{1,65},{65,1},{2,66},{66,2},{3,67},{67,3},{4,68},{68... | collective-permute-start | bytes 17301512 | tf_op jit(solution)/shard_map/ppermute | solution.py:86
  408.5 28.9 %collective-permute-start.4 = (bf16[2816,1024]{1,0:T(8,128)(2,1)}, bf16[2816,1024]{1,0:T(8,128)(2,1)S(1)}, u32[]{:S(2)}, u32[]{:S(2)}) collective-permute-start(bf16[2816,1024]{1,0:T(8,128)(2,1)} %param.20), channel_id=1, source_target_pairs={{0,64},{64,0},{1,65},{65,1},{2,66},{66,2},{3,67},{67,3},{4,68},{68... | collective-permute-start | bytes 17301512 | tf_op jit(solution)/shard_map/ppermute | solution.py:86
  422.7 12.2 %slice-start = ((s8[5767168]{0:T(1024)(128)(4,1)}), s8[4194304]{0:T(1024)(128)(4,1)S(1)}, s32[]{:S(2)}) async-start(s8[5767168]{0:T(1024)(128)(4,1)} %bitcast.89), calls=%async_computation.2 | async-start | bytes 8388608
  427.2 7.7 %slice-start.1 = ((s8[5767168]{0:T(1024)(128)(4,1)}), s8[1572864]{0:T(1024)(128)(4,1)S(1)}, s32[]{:S(2)}) async-start(s8[5767168]{0:T(1024)(128)(4,1)} %bitcast.89), calls=%async_computation.3 | async-start | bytes 3145728
  437.3 166.7 %copy-start.3 = (bf16[384,2048]{1,0:T(8,128)(2,1)S(1)}, bf16[384,2048]{1,0:T(8,128)(2,1)}, u32[]{:S(2)}) copy-start(bf16[384,2048]{1,0:T(8,128)(2,1)} %copy-done.2) | copy-start | bytes 4718596
  437.3 166.6 %copy-start.8 = (s32[384]{0:T(512)S(1)}, s32[384]{0:T(512)}, u32[]{:S(2)}) copy-start(s32[384]{0:T(512)} %copy-done.7) | copy-start | bytes 4612
  437.3 166.6 %copy-start.10 = (s32[384]{0:T(512)S(1)}, s32[384]{0:T(512)}, u32[]{:S(2)}) copy-start(s32[384]{0:T(512)} %copy-done.9) | copy-start | bytes 4612
  437.3 166.6 %copy-start.12 = (s32[384]{0:T(512)S(1)}, s32[384]{0:T(512)}, u32[]{:S(2)}) copy-start(s32[384]{0:T(512)} %copy-done.11) | copy-start | bytes 4612
  437.4 166.6 %copy-start.14 = (s32[384]{0:T(512)S(1)}, s32[384]{0:T(512)}, u32[]{:S(2)}) copy-start(s32[384]{0:T(512)} %copy-done.13) | copy-start | bytes 4612
  437.4 166.6 %copy-start.16 = (s32[384]{0:T(512)S(1)}, s32[384]{0:T(512)}, u32[]{:S(2)}) copy-start(s32[384]{0:T(512)} %get-tuple-element.9) | copy-start | bytes 4612
  437.4 166.6 %copy-start.18 = (s32[384]{0:T(512)S(1)}, s32[384]{0:T(512)}, u32[]{:S(2)}) copy-start(s32[384]{0:T(512)} %get-tuple-element.10) | copy-start | bytes 4612
  (1 other events, 1.1 us)

commit v2 on v1

--- a/solution.py
+++ b/solution.py
@@ -1,11 +1,21 @@
+import functools
+
 import jax
 import jax.numpy as jnp
 from jax import lax
+from jax.experimental import pallas as pl
+from jax.experimental.pallas import tpu as pltpu
 from jax.sharding import PartitionSpec as P
 
 HEAD_DIM = 128
 ROPE_BASE = 10000.0
 EPSILON = 1e-6
+RING = 4
+BLOCK = 8
+TURNS = 3
+WIDE = 256
+MESH = pl.DeviceIdType.MESH
+STRIDES = (RING * RING, RING, 1)
 
 
 def rms_norm(values):
@@ -68,6 +78,200 @@
     return ((5 * n_tokens * top_k) // (4 * n_experts) + 7) // 8 * 8
 
 
+def ring_peer(me, axis, offset):
+    stride = STRIDES[axis]
+    place = lax.rem(me // stride, RING)
+    return me + (lax.rem(place + offset + RING, RING) - place) * stride
+
+
+class Exchange:
+    def __init__(self, me, axes, sign, first, second, third, last, send, recv):
+        self.me, self.axes, self.sign = me, axes, sign
+        self.first, self.second, self.third, self.last = first, second, third, last
+        self.send, self.recv = send, recv
+
+    def push(self, phase, step, pairs):
+        peer = ring_peer(self.me, self.axes[phase], self.sign * step)
+        for src, dst in pairs:
+            pltpu.make_async_remote_copy(src_ref=src, dst_ref=dst, send_sem=self.send.at[phase], recv_sem=self.recv.at[phase],
+                                         device_id={"ep": peer}, device_id_type=MESH).start()
+
+    def start(self, phase):
+        for d in (1, 3, 2):
+            if phase == 0:
+                pairs = [(self.first.at[d], self.second.at[:, :, d - 1])]
+            elif phase == 1:
+                pairs = [(self.first.at[0, d], self.third.at[:, d - 1, 0]), (self.second.at[d], self.third.at[:, d - 1, pl.ds(1, 3)])]
+            else:
+                pairs = [(self.first.at[0, 0, d], self.last.at[d - 1, 0, 0]), (self.second.at[0, d], self.last.at[d - 1, 0, pl.ds(1, 3)]),
+                         (self.third.at[d], self.last.at[d - 1, pl.ds(1, 3)])]
+            self.push(phase, d, pairs)
+
+    def landing(self, phase):
+        return (self.second, self.third, self.last)[phase]
+
+    def wait_recv(self, phase):
+        whole = self.landing(phase)
+        pltpu.make_async_copy(whole, whole, self.recv.at[phase]).wait()
+
+    def wait_send(self, phase):
+        whole = self.landing(phase)
+        pltpu.make_async_copy(whole, whole, self.send.at[phase]).wait()
+
+    def kept(self):
+        return [(self.third.at[0], (0, pl.ds(1, 3))), (self.second.at[0, 0], (0, 0, pl.ds(1, 3))), (self.first.at[0, 0, 0], (0, 0, 0))]
+
+
+def moe_kernel(n_units, rows_hbm, gate_a, gate_b, up_a, up_b, down_a, down_b, done_hbm,
+               out1, out2, out3, made_hbm, back1, back2,
+               ga, gb, ua, ub, da, db, x_ref, act_ref, y_ref, w_sem, x_sem, y_sem, fill_sem, go_send, go_recv, come_send, come_recv):
+    me = lax.axis_index("ep")
+    fs = lax.axis_index("fsdp")
+    barrier = pltpu.get_barrier_semaphore()
+    for axis in range(3):
+        for d in range(1, RING):
+            pl.semaphore_signal(barrier, inc=1, device_id={"ep": ring_peer(me, axis, d)}, device_id_type=MESH)
+    pl.semaphore_wait(barrier, 3 * (RING - 1))
+
+    half = ga.shape[0]
+    inner = ga.shape[1]
+    rows = RING ** 3 * BLOCK
+    go, come = [], []
+    for u in range(n_units):
+        axes = tuple((u % TURNS + k) % 3 for k in range(3))
+        go.append(Exchange(me, axes, 1, rows_hbm.at[u], out1.at[u], out2.at[u], out3.at[u], go_send.at[u], go_recv.at[u]))
+        come.append(Exchange(me, axes[::-1], -1, made_hbm.at[u], back1.at[u], back2.at[u], done_hbm.at[u, pl.ds(1, 3)], come_send.at[u], come_recv.at[u]))
+    batches = [range(b * TURNS, (b + 1) * TURNS) for b in range(n_units // TURNS)]
+
+    for units in batches:
+        for u in units:
+            go[u].start(0)
+    weights = [pltpu.make_async_copy(src, dst, w_sem.at[n]) for n, (src, dst) in enumerate(
+        ((gate_a, ga), (gate_b, gb), (up_a, ua), (up_b, ub), (down_a, da), (down_b, db)))]
+    for copy in weights:
+        copy.start()
+    for phase in range(2):
+        for units in batches:
+            for u in units:
+                go[u].wait_recv(phase)
+                go[u].start(phase + 1)
+    for copy in weights:
+        copy.wait()
+
+    def x_copies(u):
+        slot = u % 2
+        pieces = [(go[u].last, (pl.ds(1, 3),))] + go[u].kept()
+        return [pltpu.make_async_copy(src, x_ref.at[(slot, *place)], x_sem.at[slot, n]) for n, (src, place) in enumerate(pieces)]
+
+    def y_copy(u):
+        return pltpu.make_async_copy(y_ref.at[u % 2], made_hbm.at[u], y_sem.at[u % 2])
+
+    def fetch(u):
+        go[u].wait_recv(2)
+        for copy in x_copies(u):
+            copy.start()
+
+    def expert(u):
+        slot = u % 2
+        x2 = x_ref.at[slot].reshape(rows, 2 * half)
+        y2 = y_ref.at[slot].reshape(rows, 2 * half)
+
+        def own(side):
+            return pl.ds(pl.multiple_of(lax.rem(fs + side, 2) * half, half), half)
+
+        def inner_block(cols):
+            gate = dot32(x2[:, own(0)], ga[:, cols]) + dot32(x2[:, own(1)], gb[:, cols])
+            up = dot32(x2[:, own(0)], ua[:, cols]) + dot32(x2[:, own(1)], ub[:, cols])
+            act_ref[:, cols] = (jax.nn.silu(gate) * up).astype(jnp.bfloat16)
+
+        def inner_step(n, carry):
+            inner_block(pl.ds(pl.multiple_of(n * WIDE, WIDE), WIDE))
+            return carry
+
+        whole = inner // WIDE
+        lax.fori_loop(0, whole, inner_step, 0)
+        if inner % WIDE:
+            inner_block(pl.ds(whole * WIDE, inner % WIDE))
+
+        def down_step(n, carry):
+            cols = pl.ds(pl.multiple_of(n * WIDE, WIDE), WIDE)
+            for side, weight in enumerate((da, db)):
+                target = pl.ds(pl.multiple_of(lax.rem(fs + side, 2) * half + n * WIDE, WIDE), WIDE)
+                y2[:, target] = dot32(act_ref[...], weight[:, cols]).astype(jnp.bfloat16)
+            return carry
+
+        lax.fori_loop(0, half // WIDE, down_step, 0)
+
+    fetch(0)
+    for u in range(n_units):
+        for copy in x_copies(u):
+            copy.wait()
+        if u + 1 < n_units:
+            fetch(u + 1)
+        if u >= 2:
+            pass
+        expert(u)
+        y_copy(u).start()
+        y_copy(u).wait()
+        come[u].start(0)
+    for phase in range(2):
+        for units in batches:
+            for u in units:
+                come[u].wait_recv(phase)
+                come[u].start(phase + 1)
+
+    def fill(u):
+        slot = u % 2
+        return [(pltpu.make_async_copy(src, x_ref.at[(slot, *place)], fill_sem.at[slot, n]),
+                 pltpu.make_async_copy(x_ref.at[(slot, *place)], done_hbm.at[(u, *place)], fill_sem.at[slot, n])) for n, (src, place) in enumerate(come[u].kept())]
+
+    for u in range(n_units):
+        copies = fill(u)
+        for load, _ in copies:
+            load.start()
+        for load, store in copies:
+            load.wait()
+            store.start()
+        for _, store in copies:
+            store.wait()
+    for u in range(n_units):
+        come[u].wait_recv(2)
+    for u in range(n_units):
+        for phase in range(3):
+            go[u].wait_send(phase)
+            come[u].wait_send(phase)
+
+
+def moe_exchange(rows, gate_pair, up_pair, down_pair):
+    n_units, width = rows.shape[0], rows.shape[-1]
+    anywhere = pl.BlockSpec(memory_space=pl.ANY)
+    weights = (*gate_pair, *up_pair, *down_pair)
+    inner = gate_pair[0].shape[1]
+
+    def blocks(*lead):
+        return jax.ShapeDtypeStruct((n_units, *lead, BLOCK, width), jnp.bfloat16)
+
+    cube = (RING, RING, RING, BLOCK, width)
+    outs = (blocks(4, 4, 4), blocks(4, 4, 3), blocks(4, 3, 4), blocks(3, 4, 4), blocks(4, 4, 4), blocks(4, 4, 3), blocks(4, 3, 4))
+    sems = pltpu.SemaphoreType.DMA
+    return pl.pallas_call(
+        functools.partial(moe_kernel, n_units),
+        out_shape=outs,
+        in_specs=[anywhere] * 7,
+        out_specs=(anywhere,) * 7,
+        scratch_shapes=[pltpu.VMEM(w.shape, jnp.bfloat16) for w in weights] + [
+            pltpu.VMEM((2, *cube), jnp.bfloat16),
+            pltpu.VMEM((RING ** 3 * BLOCK, inner), jnp.bfloat16),
+            pltpu.VMEM((2, *cube), jnp.bfloat16),
+            sems((6,)), sems((2, 4)), sems((2,)), sems((2, 3)),
+            sems((n_units, 3)), sems((n_units, 3)), sems((n_units, 3)), sems((n_units, 3)),
+        ],
+        compiler_params=pltpu.CompilerParams(collective_id=0, has_side_effects=True, vmem_limit_bytes=48 * 1024 * 1024),
+        cost_estimate=pl.CostEstimate(flops=250_000_000_000, bytes_accessed=100_000_000, transcendentals=0),
+        name="moe_exchange",
+    )(rows, *weights)[0]
+
+
 def solution(mesh):
     n_ep = mesh.shape["ep"]
     tok_spec = P(("data", "fsdp", "ep"))
@@ -91,7 +295,15 @@
 
         ids_flat = expert_ids.reshape(n_tokens, top_k)
         slots_flat = slot_ids.reshape(n_tokens, top_k)
-        row_of = jnp.where(slots_flat >= 0, ids_flat * capacity + slots_flat, -1)
+        me = lax.axis_index("ep")
+        rel = [lax.rem(ids_flat // s - me // s + n_ep, RING) for s in STRIDES]
+        unit, within = slots_flat // BLOCK, slots_flat % BLOCK
+        turn = unit % TURNS
+        place = jnp.zeros_like(slots_flat)
+        for r in range(TURNS):
+            order = [rel[(r + k) % 3] for k in range(3)]
+            place = jnp.where(turn == r, (order[0] * RING + order[1]) * RING + order[2], place)
+        row_of = jnp.where(slots_flat >= 0, (unit * n_experts + place) * BLOCK + within, -1)
         row_iota = jnp.arange(n_rows, dtype=jnp.int32)
         gates = gate_vals.reshape(n_tokens, top_k)
         picks = sum((row_iota[:, None] == row_of[None, :, k]).astype(jnp.bfloat16) for k in range(top_k))
@@ -99,17 +311,14 @@
 
         hidden = attention_block(x_in, qkv_pair, out_pair, fs)
         normed = rms_norm(hidden)
-        buffer = dot32(picks, normed).astype(jnp.bfloat16).reshape(n_experts, capacity, model_dim)
-        received = lax.all_to_all(buffer, "ep", 0, 0, tiled=True).reshape(n_rows, model_dim)
+        buffer = dot32(picks, normed).astype(jnp.bfloat16)
+        rows = buffer.reshape(capacity // BLOCK, RING, RING, RING, BLOCK, model_dim)
 
         halves = split_cols(normed, fs)
         shared_act = (jax.nn.silu(paired_dot(halves, sgate_pair)) * paired_dot(halves, sup_pair)).astype(jnp.bfloat16)
         base = hidden.astype(jnp.float32) + join_cols(shared_act, sdown_pair, fs)
 
-        got = split_cols(received, fs)
-        act = (jax.nn.silu(paired_dot(got, gate_pair)) * paired_dot(got, up_pair)).astype(jnp.bfloat16)
-        expert_out = join_cols(act, down_pair, fs).astype(jnp.bfloat16).reshape(n_experts, capacity, model_dim)
-        returned = lax.all_to_all(expert_out, "ep", 0, 0, tiled=True).reshape(n_rows, model_dim)
+        returned = moe_exchange(rows, gate_pair, up_pair, down_pair).reshape(n_rows, model_dim)
         summed = base + dot32(spread, returned)
         return summed.astype(jnp.bfloat16).reshape(n_batch, seq_len, model_dim)
 

time: 629 us -> 447 us (0.71)
  the two profiles are of different devices: /device:TPU:8 before, /device:TPU:0 now
where the time goes in v2:
time: 447 us; the launch traced here: 442 us
  Pallas kernels  318 us (71%)
  matrix products  91 us (20%)
  other arithmetic  14.1 us (3%)
  local copies, waits for them, and re-layouts  10.7 us (2%)
  waiting for transfers between devices  4.67 us (1%)
    pallas_call x1, Pallas kernels, moe_exchange(): pl.pallas_call(functools.partial(moe_kernel, n_units), out_shape=outs, in...  318 us
    dot_general x12, matrix products, dot32(): return jnp.dot(left, right, preferred_element_type=jnp.float32)  81.2 us
  transfers between devices with their start and end apart: 8, of which 1 were waited for; matrix products, arithmetic and copies ran while one was open for 23% of the time, Pallas kernels for 0%

profile of v2, /device:TPU:0, one launch (start us, length us, event | category | flops | bytes accessed | tf_op | source)
XLA Modules:
  0.0 442.0 jit_solution(16294774513068365514)
XLA Ops:
  0.0 0.5 collective-permute-start.1
  0.5 0.5 collective-permute-start.2
  1.0 1.5 slice_reduce_fusion.10
  2.6 0.8 fusion.111
  3.5 1.8 fusion.24
  5.3 0.7 fusion.100
  6.4 8.0 %fusion.85 = f32[384,6144]{1,0:T(8,128)S(1)} fusion(bf16[1024,6144]{1,0:T(8,128)(2,1)} %param.13, bf16[1,384,2048]{2,1,0:T(8,128)(2,1)S(1)} %fusion.25, s32[]{:T(128)S(6)} %select_n.86), kind=kOutput, calls=%fused_computation.104 | convolution fusion | flops 4831838208 | bytes 22806532 | tf_op jit(solution)/shard_map/dot_general | solution.py:41
  14.5 4.6 %collective-permute-done = bf16[1024,6144]{1,0:T(8,128)(2,1)} collective-permute-done((bf16[1024,6144]{1,0:T(8,128)(2,1)}, bf16[1024,6144]{1,0:T(8,128)(2,1)}, u32[]{:S(2)}, u32[]{:S(2)}) %collective-permute-start) | collective-permute-done | bytes 12582944 | tf_op jit(solution)/shard_map/ppermute | solution.py:290
  19.4 10.3 %fusion.61 = bf16[48,8,48,128]{3,1,2,0:T(8,128)(2,1)S(1)} fusion(f32[384,6144]{1,0:T(8,128)S(1)} %fusion.85, bf16[1024,6144]{1,0:T(8,128)(2,1)} %collective-permute-done, bf16[1,384,2048]{2,1,0:T(8,128)(2,1)S(1)} %fusion.25, s32[]{:T(128)S(6)} %select_n.87), kind=kOutput, calls=%fused_computation.78 | convolution fusion | flops 4836556800 | bytes 27525124 | tf_op jit(solution)/shard_map/dot_general | solution.py:41
  29.7 1.3 copy.23
  31.0 2.0 fusion.129
  32.9 0.8 fusion.74
  33.7 4.0 fusion.65
  37.7 2.9 copy.20
  40.6 4.7 %fusion.67 = f32[16,384,384]{1,2,0:T(8,128)S(1)} fusion(bf16[384,16,64]{2,0,1:T(8,128)(2,1)} %get-tuple-element.26, bf16[384,16,64]{2,0,1:T(8,128)(2,1)} %get-tuple-element.27, bf16[384,16,64]{2,0,1:T(8,128)(2,1)} %get-tuple-element.23, bf16[384,16,64]{2,0,1:T(8,128)(2,1)} %get-tuple-element.22), kind=kOutput, calls=%fused_computation.84 | convolution fusion | flops 610271232 | bytes 12582912 | tf_op jit(solution)/shard_map/bqhd,bkhd->bhqk/dot_general | solution.py:69
  45.3 5.3 %fusion.130 = (f32[16,384]{1,0:T(8,128)S(1)}, f32[16,384,384]{1,2,0:T(8,128)}) fusion(f32[16,384,384]{1,2,0:T(8,128)S(1)} %fusion.67, pred[384,384]{0,1:T(8,128)(4,1)S(1)} %iota_compare_fusion.12), kind=kOutput, calls=%fused_computation.192 | output fusion | flops 14156159 | bytes 19046400 | tf_op jit(solution)/shard_map/sub | solution.py:71
  50.7 5.1 %fusion.62 = bf16[16,128,384]{2,1,0:T(8,128)(2,1)S(1)} fusion(f32[16,384,384]{1,2,0:T(8,128)} %get-tuple-element.31, f32[16,384]{1,0:T(8,128)S(1)} %get-tuple-element.30, bf16[1,384,1,16,128]{1,4,3,2,0:T(8,128)(2,1)S(1)} %copy-done.6), kind=kOutput, calls=%fused_computation.79 | convolution fusion | flops 609484800 | bytes 12607488 | tf_op jit(solution)/shard_map/bhqk,bkhd->bqhd/dot_general | solution.py:72
  55.9 1.9 fusion.88
  58.2 4.7 %fusion.18 = (f32[384]{0:T(512)S(1)}, bf16[384,2048]{1,0:T(8,128)(2,1)S(1)}) fusion(f32[384,2048]{1,0:T(8,128)S(1)} %fusion.88, bf16[1024,2048]{1,0:T(8,128)(2,1)} %collective-permute-done.1, bf16[384,2048]{0,1:T(8,128)(2,1)S(1)} %bitcast.114, s32[]{:T(128)S(6)} %select_n.87, bf16[1,384,2048]{2,1,0:T(8,128)(2,1)S(1)} %copy-done.2), kind=kOutput, calls=%fused_computation.42 | convolution fusion | flops 1616117376 | bytes 11273732 | tf_op jit(solution)/shard_map/dot_general | solution.py:41
  63.3 2.4 fusion.95
  65.7 0.4 slice-done.1
  66.1 2.4 fusion.97
  68.5 0.7 collective-permute-start.7
  69.2 7.0 %fusion.93 = f32[384,2816]{1,0:T(8,128)} fusion(bf16[1024,2816]{1,0:T(8,128)(2,1)} %collective-permute-done.2, bf16[384,2048]{1,0:T(8,128)(2,1)S(1)} %fusion.19, s32[]{:T(128)S(6)} %select_n.87), kind=kOutput, calls=%fused_computation.112 | convolution fusion | flops 2214592512 | bytes 10878980 | tf_op jit(solution)/shard_map/dot_general | solution.py:41
  76.3 6.8 %multiply_convert_fusion = bf16[384,2816]{1,0:T(8,128)(2,1)S(1)} fusion(f32[384,2816]{1,0:T(8,128)S(1)} %fusion.95, f32[384,2816]{1,0:T(8,128)S(1)} %fusion.97, f32[384,2816]{1,0:T(8,128)} %fusion.93, bf16[1024,2816]{1,0:T(8,128)(2,1)} %collective-permute-done.3, bf16[384,2048]{1,0:T(8,128)(2,1)S(1)} %fusion.19, s32[]{:T(128)S(6)} %select_n.87), kind=kOutput, calls=%fused_computation.41 | convolution fusion | flops 2223243264 | bytes 21692420 | tf_op jit(solution)/shard_map/dot_general | solution.py:41
  83.1 6.2 %fusion.131 = f32[384,1024]{1,0:T(8,128)} fusion(bf16[384,2816]{1,0:T(8,128)(2,1)S(1)} %multiply_convert_fusion, bf16[2816,1024]{1,0:T(8,128)(2,1)} %param.20), kind=kOutput, calls=%fused_computation.193 | convolution fusion | flops 2214592512 | bytes 9502720 | tf_op jit(solution)/shard_map/dot_general | solution.py:41
  89.3 6.3 %fusion.132 = f32[384,1024]{1,0:T(8,128)} fusion(bf16[384,2816]{1,0:T(8,128)(2,1)S(1)} %multiply_convert_fusion, bf16[2816,1024]{1,0:T(8,128)(2,1)} %collective-permute-done.4), kind=kOutput, calls=%fused_computation.194 | convolution fusion | flops 2214592512 | bytes 9502720 | tf_op jit(solution)/shard_map/dot_general | solution.py:41
  95.7 11.8 %convolution_convert_fusion = bf16[3072,2048]{1,0:T(8,128)(2,1)} fusion(bf16[384,2048]{1,0:T(8,128)(2,1)S(1)} %fusion.19, s32[384]{0:T(512)S(1)} %get-tuple-element.8, s32[384]{0:T(512)S(1)} %get-tuple-element.9, s32[384]{0:T(512)S(1)} %get-tuple-element.10, s32[384]{0:T(512)S(1)} %get-tuple-element.11, s32[384]{0:T(512)S(1)} %get-tuple-element.12, ...), kind=kOutput, calls=%fused_computation.1 | convolution fusion | flops 4866441216 | bytes 14164992 | tf_op jit(solution)/shard_map/dot_general | solution.py:41
  107.5 1.6 copy-done.28
  109.1 0.8 copy-done.27
  110.0 318.1 %moe_exchange.1 = (bf16[6,4,4,4,8,2048]{5,4,3,2,1,0:T(8,128)(2,1)}, bf16[6,4,4,3,8,2048]{5,4,3,2,1,0:T(8,128)(2,1)}, bf16[6,4,3,4,8,2048]{5,4,3,2,1,0:T(8,128)(2...) custom-call(bf16[6,4,4,4,8,2048]{5,4,3,2,1,0:T(8,128)(2,1)} %bitcast, ...), custom_call_target="tpu_custom_call" | custom-call | flops 249999998976 | bytes 100000000 | tf_op jit(solution)/shard_map/moe_exchange/pallas_call | solution.py:257
  428.3 13.4 %fusion.26 = bf16[1,384,2048]{2,1,0:T(8,128)(2,1)} fusion(bf16[3072,2048]{1,0:T(8,128)(2,1)} %bitcast.124, f32[384,1024]{1,0:T(8,128)S(1)} %copy-done.29, f32[384,1024]{1,0:T(8,128)S(1)} %copy-done.30, bf16[384,2048]{1,0:T(8,128)(2,1)S(1)} %copy-done.5, s32[384]{0:T(512)S(1)} %copy-done.10, s32[384]{0:T(512)S(1)} %copy-done.12, s32[384]{0:T(512)S(1)} %copy-done.14, ...), kind=kOutput, calls=%fused_computation.55 | convolution fusion | flops 4865654784 | bytes 18888192 | tf_op jit(solution)/shard_map/dot_general | solution.py:41
  (88 shorter events, 1.7 us)
Async XLA Ops:
  0.0 19.1 %collective-permute-start = (bf16[1024,6144]{1,0:T(8,128)(2,1)}, bf16[1024,6144]{1,0:T(8,128)(2,1)}, u32[]{:S(2)}, u32[]{:S(2)}) collective-permute-start(bf16[1024,6144]{1,0:T(8,128)(2,1)} %param.13), channel_id=1, source_target_pairs={{0,64},{64,0},{1,65},{65,1},{2,66},{66,2},{3,67},{67,3},{4,68},{68... | collective-permute-start | bytes 37748744 | tf_op jit(solution)/shard_map/ppermute | solution.py:290
  0.0 57.7 %collective-permute-start.1 = (bf16[1024,2048]{1,0:T(8,128)(2,1)}, bf16[1024,2048]{1,0:T(8,128)(2,1)}, u32[]{:S(2)}, u32[]{:S(2)}) collective-permute-start(bf16[1024,2048]{1,0:T(8,128)(2,1)} %param.14), channel_id=1, source_target_pairs={{0,64},{64,0},{1,65},{65,1},{2,66},{66,2},{3,67},{67,3},{4,68},{68... | collective-permute-start | bytes 12582920 | tf_op jit(solution)/shard_map/ppermute | solution.py:290
  0.5 107.0 %collective-permute-start.5 = (bf16[1024,1408]{1,0:T(8,128)(2,1)}, bf16[1024,1408]{1,0:T(8,128)(2,1)S(1)}, u32[]{:S(2)}, u32[]{:S(2)}) collective-permute-start(bf16[1024,1408]{1,0:T(8,128)(2,1)} %bitcast.110), channel_id=1, source_target_pairs={{0,64},{64,0},{1,65},{65,1},{2,66},{66,2},{3,67},{67,3},{4,68},{68... | collective-permute-start | bytes 8650760 | tf_op jit(solution)/shard_map/ppermute | solution.py:290
  0.5 68.0 %collective-permute-start.2 = (bf16[1024,2816]{1,0:T(8,128)(2,1)}, bf16[1024,2816]{1,0:T(8,128)(2,1)}, u32[]{:S(2)}, u32[]{:S(2)}) collective-permute-start(bf16[1024,2816]{1,0:T(8,128)(2,1)} %param.18), channel_id=1, source_target_pairs={{0,64},{64,0},{1,65},{65,1},{2,66},{66,2},{3,67},{67,3},{4,68},{68... | collective-permute-start | bytes 17301512 | tf_op jit(solution)/shard_map/ppermute | solution.py:290
  1.0 75.3 %collective-permute-start.3 = (bf16[1024,2816]{1,0:T(8,128)(2,1)}, bf16[1024,2816]{1,0:T(8,128)(2,1)}, u32[]{:S(2)}, u32[]{:S(2)}) collective-permute-start(bf16[1024,2816]{1,0:T(8,128)(2,1)} %param.19), channel_id=1, source_target_pairs={{0,64},{64,0},{1,65},{65,1},{2,66},{66,2},{3,67},{67,3},{4,68},{68... | collective-permute-start | bytes 17301512 | tf_op jit(solution)/shard_map/ppermute | solution.py:290
  3.4 92.2 %copy-start.7 = (s32[384]{0:T(512)}, s32[384]{0:T(512)S(1)}, u32[]{:S(2)}) copy-start(s32[384]{0:T(512)S(1)} %get-tuple-element.7) | copy-start | bytes 4612
  3.4 92.2 %copy-start.9 = (s32[384]{0:T(512)}, s32[384]{0:T(512)S(1)}, u32[]{:S(2)}) copy-start(s32[384]{0:T(512)S(1)} %get-tuple-element.8) | copy-start | bytes 4612
  3.4 92.2 %copy-start.11 = (s32[384]{0:T(512)}, s32[384]{0:T(512)S(1)}, u32[]{:S(2)}) copy-start(s32[384]{0:T(512)S(1)} %get-tuple-element.9) | copy-start | bytes 4612
  3.4 92.2 %copy-start.13 = (s32[384]{0:T(512)}, s32[384]{0:T(512)S(1)}, u32[]{:S(2)}) copy-start(s32[384]{0:T(512)S(1)} %get-tuple-element.10) | copy-start | bytes 4612
  3.4 92.2 %copy-start.15 = (s32[384]{0:T(512)}, s32[384]{0:T(512)S(1)}, u32[]{:S(2)}) copy-start(s32[384]{0:T(512)S(1)} %get-tuple-element.11) | copy-start | bytes 4612
  3.5 92.2 %copy-start.17 = (s32[384]{0:T(512)}, s32[384]{0:T(512)S(1)}, u32[]{:S(2)}) copy-start(s32[384]{0:T(512)S(1)} %get-tuple-element.12) | copy-start | bytes 4612
  19.1 70.2 %collective-permute-start.4 = (bf16[2816,1024]{1,0:T(8,128)(2,1)}, bf16[2816,1024]{1,0:T(8,128)(2,1)}, u32[]{:S(2)}, u32[]{:S(2)}) collective-permute-start(bf16[2816,1024]{1,0:T(8,128)(2,1)} %param.20), channel_id=1, source_target_pairs={{0,64},{64,0},{1,65},{65,1},{2,66},{66,2},{3,67},{67,3},{4,68},{68... | collective-permute-start | bytes 17301512 | tf_op jit(solution)/shard_map/ppermute | solution.py:290
  57.7 5.5 %slice-start.2 = ((s8[5767168]{0:T(1024)(128)(4,1)}), s8[4194304]{0:T(1024)(128)(4,1)S(1)}, s32[]{:S(2)}) async-start(s8[5767168]{0:T(1024)(128)(4,1)} %bitcast.118), calls=%async_computation.2 | async-start | bytes 8388608
  57.8 5.5 %slice-start.3 = ((s8[5767168]{0:T(1024)(128)(4,1)}), s8[1572864]{0:T(1024)(128)(4,1)S(1)}, s32[]{:S(2)}) async-start(s8[5767168]{0:T(1024)(128)(4,1)} %bitcast.118), calls=%async_computation.3 | async-start | bytes 3145728
  57.8 49.7 %collective-permute-start.6 = (bf16[1024,1408]{1,0:T(8,128)(2,1)S(1)}, bf16[1024,1408]{1,0:T(8,128)(2,1)S(1)}, u32[]{:S(2)}, u32[]{:S(2)}) collective-permute-start(bf16[1024,1408]{1,0:T(8,128)(2,1)S(1)} %bitcast.121), channel_id=1, source_target_pairs={{0,64},{64,0},{1,65},{65,1},{2,66},{66,2},{3,67},{67,3},{4,68},{68... | collective-permute-start | bytes 8650760 | tf_op jit(solution)/shard_map/ppermute | solution.py:290
  68.5 39.0 %collective-permute-start.7 = (bf16[1408,1024]{1,0:T(8,128)(2,1)S(1)}, bf16[1408,1024]{1,0:T(8,128)(2,1)S(1)}, u32[]{:S(2)}, u32[]{:S(2)}) collective-permute-start(bf16[1408,1024]{1,0:T(8,128)(2,1)S(1)} %bitcast.123), channel_id=1, source_target_pairs={{0,64},{64,0},{1,65},{65,1},{2,66},{66,2},{3,67},{67,3},{4,68},{68... | collective-permute-start | bytes 8650760 | tf_op jit(solution)/shard_map/ppermute | solution.py:290
  95.7 14.3 %copy-start = (bf16[1,1024,1408]{2,1,0:T(8,128)(2,1)S(1)}, bf16[1,1024,1408]{2,1,0:T(8,128)(2,1)}, u32[]{:S(2)}) copy-start(bf16[1,1024,1408]{2,1,0:T(8,128)(2,1)} %param.15) | copy-start | bytes 8650756
  109.9 318.3 %copy-start.5 = (bf16[384,2048]{1,0:T(8,128)(2,1)S(1)}, bf16[384,2048]{1,0:T(8,128)(2,1)}, u32[]{:S(2)}) copy-start(bf16[384,2048]{1,0:T(8,128)(2,1)} %copy-done.4) | copy-start | bytes 4718596
  109.9 318.3 %copy-start.8 = (s32[384]{0:T(512)S(1)}, s32[384]{0:T(512)}, u32[]{:S(2)}) copy-start(s32[384]{0:T(512)} %copy-done.7) | copy-start | bytes 4612
  109.9 318.3 %copy-start.10 = (s32[384]{0:T(512)S(1)}, s32[384]{0:T(512)}, u32[]{:S(2)}) copy-start(s32[384]{0:T(512)} %copy-done.9) | copy-start | bytes 4612
  109.9 318.3 %copy-start.12 = (s32[384]{0:T(512)S(1)}, s32[384]{0:T(512)}, u32[]{:S(2)}) copy-start(s32[384]{0:T(512)} %copy-done.11) | copy-start | bytes 4612
  109.9 318.3 %copy-start.14 = (s32[384]{0:T(512)S(1)}, s32[384]{0:T(512)}, u32[]{:S(2)}) copy-start(s32[384]{0:T(512)} %copy-done.13) | copy-start | bytes 4612
  109.9 318.3 %copy-start.16 = (s32[384]{0:T(512)S(1)}, s32[384]{0:T(512)}, u32[]{:S(2)}) copy-start(s32[384]{0:T(512)} %copy-done.15) | copy-start | bytes 4612
  110.0 318.3 %copy-start.18 = (s32[384]{0:T(512)S(1)}, s32[384]{0:T(512)}, u32[]{:S(2)}) copy-start(s32[384]{0:T(512)} %copy-done.17) | copy-start | bytes 4612
  110.0 318.3 %copy-start.19 = (bf16[384]{0:T(512)(128)(2,1)S(1)}, bf16[384]{0:T(512)(128)(2,1)}, u32[]{:S(2)}) copy-start(bf16[384]{0:T(512)(128)(2,1)} %get-tuple-element.13) | copy-start | bytes 2308
  110.0 318.3 %copy-start.20 = (bf16[384]{0:T(512)(128)(2,1)S(1)}, bf16[384]{0:T(512)(128)(2,1)}, u32[]{:S(2)}) copy-start(bf16[384]{0:T(512)(128)(2,1)} %get-tuple-element.14) | copy-start | bytes 2308
  110.0 318.3 %copy-start.21 = (bf16[384]{0:T(512)(128)(2,1)S(1)}, bf16[384]{0:T(512)(128)(2,1)}, u32[]{:S(2)}) copy-start(bf16[384]{0:T(512)(128)(2,1)} %get-tuple-element.15) | copy-start | bytes 2308
  110.0 318.3 %copy-start.22 = (bf16[384]{0:T(512)(128)(2,1)S(1)}, bf16[384]{0:T(512)(128)(2,1)}, u32[]{:S(2)}) copy-start(bf16[384]{0:T(512)(128)(2,1)} %get-tuple-element.16) | copy-start | bytes 2308
  110.0 318.3 %copy-start.23 = (bf16[384]{0:T(512)(128)(2,1)S(1)}, bf16[384]{0:T(512)(128)(2,1)}, u32[]{:S(2)}) copy-start(bf16[384]{0:T(512)(128)(2,1)} %get-tuple-element.17) | copy-start | bytes 2308
  110.0 318.3 %copy-start.24 = (bf16[384]{0:T(512)(128)(2,1)S(1)}, bf16[384]{0:T(512)(128)(2,1)}, u32[]{:S(2)}) copy-start(bf16[384]{0:T(512)(128)(2,1)} %get-tuple-element.18) | copy-start | bytes 2308
  110.0 318.3 %copy-start.29 = (f32[384,1024]{1,0:T(8,128)S(1)}, f32[384,1024]{1,0:T(8,128)}, u32[]{:S(2)}) copy-start(f32[384,1024]{1,0:T(8,128)} %fusion.131) | copy-start | bytes 4718596
  110.0 318.3 %copy-start.30 = (f32[384,1024]{1,0:T(8,128)S(1)}, f32[384,1024]{1,0:T(8,128)}, u32[]{:S(2)}) copy-start(f32[384,1024]{1,0:T(8,128)} %fusion.132) | copy-start | bytes 4718596
  (11 other events, 34.8 us)

commit v3 on v2

--- a/solution.py
+++ b/solution.py
@@ -50,11 +50,6 @@
 
 def paired_dot(own_other, pair):
     return dot32(own_other[0], pair[0]) + dot32(own_other[1], pair[1])
-
-
-def join_cols(left, pair, fs):
-    own, other = dot32(left, pair[0]), dot32(left, pair[1])
-    return jnp.where(fs == 0, jnp.concatenate([own, other], axis=1), jnp.concatenate([other, own], axis=1))
 
 
 def attention_block(x_in, qkv_pair, out_pair, fs):
@@ -122,9 +117,11 @@
         return [(self.third.at[0], (0, pl.ds(1, 3))), (self.second.at[0, 0], (0, 0, pl.ds(1, 3))), (self.first.at[0, 0, 0], (0, 0, 0))]
 
 
-def moe_kernel(n_units, rows_hbm, gate_a, gate_b, up_a, up_b, down_a, down_b, done_hbm,
-               out1, out2, out3, made_hbm, back1, back2,
-               ga, gb, ua, ub, da, db, x_ref, act_ref, y_ref, w_sem, x_sem, y_sem, fill_sem, go_send, go_recv, come_send, come_recv):
+def moe_kernel(n_units, top_k, rows_hbm, normed_ref, hidden_ref, place_ref, weight_ref,
+               gate_a, gate_b, up_a, up_b, down_a, down_b, sgate_a, sgate_b, sup_a, sup_b, sdown_a, sdown_b, sum_ref,
+               out1, out2, out3, made_hbm, back1, back2, back3,
+               ga, gb, ua, ub, da, db, sin_ref, sdn_ref, x_ref, act_ref, y_ref, total_ref, mix_ref,
+               w_sem, s_sem, x_sem, y_sem, go_send, go_recv, come_send, come_recv):
     me = lax.axis_index("ep")
     fs = lax.axis_index("fsdp")
     barrier = pltpu.get_barrier_semaphore()
@@ -136,48 +133,88 @@
     half = ga.shape[0]
     inner = ga.shape[1]
     rows = RING ** 3 * BLOCK
+    n_tokens = normed_ref.shape[0]
     go, come = [], []
     for u in range(n_units):
         axes = tuple((u % TURNS + k) % 3 for k in range(3))
         go.append(Exchange(me, axes, 1, rows_hbm.at[u], out1.at[u], out2.at[u], out3.at[u], go_send.at[u], go_recv.at[u]))
-        come.append(Exchange(me, axes[::-1], -1, made_hbm.at[u], back1.at[u], back2.at[u], done_hbm.at[u, pl.ds(1, 3)], come_send.at[u], come_recv.at[u]))
-    batches = [range(b * TURNS, (b + 1) * TURNS) for b in range(n_units // TURNS)]
-
-    for units in batches:
-        for u in units:
-            go[u].start(0)
+        come.append(Exchange(me, axes[::-1], -1, made_hbm.at[u], back1.at[u], back2.at[u], back3.at[u], come_send.at[u], come_recv.at[u]))
+    units = range(n_units)
+    first, second = range(TURNS), range(TURNS, n_units)
+
+    def own(side):
+        return pl.ds(pl.multiple_of(lax.rem(fs + side, 2) * half, half), half)
+
+    def own_block(side, n):
+        return pl.ds(pl.multiple_of(lax.rem(fs + side, 2) * half + n * WIDE, WIDE), WIDE)
+
+    def block_at(n):
+        return pl.ds(pl.multiple_of(n * WIDE, WIDE), WIDE)
+
+    def shared_copies(n, slot):
+        pairs = [(src.at[:, block_at(n)], sin_ref.at[slot, k]) for k, src in enumerate((sgate_a, sgate_b, sup_a, sup_b))]
+        pairs += [(src.at[block_at(n)], sdn_ref.at[slot, k]) for k, src in enumerate((sdown_a, sdown_b))]
+        return [pltpu.make_async_copy(src, dst, s_sem.at[slot, k]) for k, (src, dst) in enumerate(pairs)]
+
+    for copy in shared_copies(0, 0):
+        copy.start()
+    for u in units:
+        go[u].start(0)
     weights = [pltpu.make_async_copy(src, dst, w_sem.at[n]) for n, (src, dst) in enumerate(
         ((gate_a, ga), (gate_b, gb), (up_a, ua), (up_b, ub), (down_a, da), (down_b, db)))]
     for copy in weights:
         copy.start()
+    total_ref[...] = hidden_ref[...].astype(jnp.float32)
+
+    n_shared = sgate_a.shape[1] // WIDE
+
+    def shared_step(n, carry):
+        slot = lax.rem(n, 2)
+        for copy in shared_copies(n, slot):
+            copy.wait()
+
+        @pl.when(n + 1 < n_shared)
+        def _():
+            for copy in shared_copies(n + 1, 1 - slot):
+                copy.start()
+
+        left, right = normed_ref[:, own(0)], normed_ref[:, own(1)]
+        gate = dot32(left, sin_ref[slot, 0]) + dot32(right, sin_ref[slot, 1])
+        up = dot32(left, sin_ref[slot, 2]) + dot32(right, sin_ref[slot, 3])
+        act_ref[pl.ds(0, n_tokens), pl.ds(0, WIDE)] = (jax.nn.silu(gate) * up).astype(jnp.bfloat16)
+
+        def shared_down(m, c):
+            for side in range(2):
+                total_ref[:, own_block(side, m)] += dot32(act_ref[pl.ds(0, n_tokens), pl.ds(0, WIDE)], sdn_ref[slot, side, :, block_at(m)])
+            return c
+
+        lax.fori_loop(0, half // WIDE, shared_down, 0)
+        return carry
+
+    lax.fori_loop(0, n_shared, shared_step, 0)
+
+    def advance(exchange, phase):
+        exchange.wait_recv(phase)
+        exchange.start(phase + 1)
+
     for phase in range(2):
-        for units in batches:
-            for u in units:
-                go[u].wait_recv(phase)
-                go[u].start(phase + 1)
+        for u in units:
+            advance(go[u], phase)
     for copy in weights:
         copy.wait()
 
-    def x_copies(u):
-        slot = u % 2
-        pieces = [(go[u].last, (pl.ds(1, 3),))] + go[u].kept()
+    def loads(exchange, slot):
+        pieces = [(exchange.last, (pl.ds(1, 3),))] + exchange.kept()
         return [pltpu.make_async_copy(src, x_ref.at[(slot, *place)], x_sem.at[slot, n]) for n, (src, place) in enumerate(pieces)]
 
-    def y_copy(u):
-        return pltpu.make_async_copy(y_ref.at[u % 2], made_hbm.at[u], y_sem.at[u % 2])
-
-    def fetch(u):
-        go[u].wait_recv(2)
-        for copy in x_copies(u):
+    def fetch(exchange, slot):
+        exchange.wait_recv(2)
+        for copy in loads(exchange, slot):
             copy.start()
 
-    def expert(u):
-        slot = u % 2
+    def expert(slot):
         x2 = x_ref.at[slot].reshape(rows, 2 * half)
         y2 = y_ref.at[slot].reshape(rows, 2 * half)
-
-        def own(side):
-            return pl.ds(pl.multiple_of(lax.rem(fs + side, 2) * half, half), half)
 
         def inner_block(cols):
             gate = dot32(x2[:, own(0)], ga[:, cols]) + dot32(x2[:, own(1)], gb[:, cols])
@@ -185,7 +222,7 @@
             act_ref[:, cols] = (jax.nn.silu(gate) * up).astype(jnp.bfloat16)
 
         def inner_step(n, carry):
-            inner_block(pl.ds(pl.multiple_of(n * WIDE, WIDE), WIDE))
+            inner_block(block_at(n))
             return carry
 
         whole = inner // WIDE
@@ -194,82 +231,99 @@
             inner_block(pl.ds(whole * WIDE, inner % WIDE))
 
         def down_step(n, carry):
-            cols = pl.ds(pl.multiple_of(n * WIDE, WIDE), WIDE)
             for side, weight in enumerate((da, db)):
-                target = pl.ds(pl.multiple_of(lax.rem(fs + side, 2) * half + n * WIDE, WIDE), WIDE)
-                y2[:, target] = dot32(act_ref[...], weight[:, cols]).astype(jnp.bfloat16)
+                y2[:, own_block(side, n)] = dot32(act_ref[...], weight[:, block_at(n)]).astype(jnp.bfloat16)
             return carry
 
         lax.fori_loop(0, half // WIDE, down_step, 0)
 
-    fetch(0)
-    for u in range(n_units):
-        for copy in x_copies(u):
+    fetch(go[0], 0)
+    for u in units:
+        slot = u % 2
+        for copy in loads(go[u], slot):
             copy.wait()
         if u + 1 < n_units:
-            fetch(u + 1)
-        if u >= 2:
-            pass
-        expert(u)
-        y_copy(u).start()
-        y_copy(u).wait()
+            fetch(go[u + 1], 1 - slot)
+        expert(slot)
+        copy = pltpu.make_async_copy(y_ref.at[slot], made_hbm.at[u], y_sem.at[slot])
+        copy.start()
+        copy.wait()
         come[u].start(0)
-    for phase in range(2):
-        for units in batches:
-            for u in units:
-                come[u].wait_recv(phase)
-                come[u].start(phase + 1)
-
-    def fill(u):
-        slot = u % 2
-        return [(pltpu.make_async_copy(src, x_ref.at[(slot, *place)], fill_sem.at[slot, n]),
-                 pltpu.make_async_copy(x_ref.at[(slot, *place)], done_hbm.at[(u, *place)], fill_sem.at[slot, n])) for n, (src, place) in enumerate(come[u].kept())]
-
-    for u in range(n_units):
-        copies = fill(u)
-        for load, _ in copies:
-            load.start()
-        for load, store in copies:
-            load.wait()
-            store.start()
-        for _, store in copies:
-            store.wait()
-    for u in range(n_units):
-        come[u].wait_recv(2)
-    for u in range(n_units):
+        if u == n_units - 3:
+            advance(come[0], 0)
+        if u == n_units - 2:
+            advance(come[1], 0)
+            advance(come[2], 0)
+    for u in second:
+        advance(come[u], 0)
+    for u in units:
+        advance(come[u], 1)
+
+    def mix(u, slot):
+        for c in range(rows // 128):
+            at = lax.broadcasted_iota(jnp.int32, (n_tokens, 128), 1) + (u * rows + c * 128)
+            part = jnp.zeros((n_tokens, 128), jnp.float32)
+            for k in range(top_k):
+                part += jnp.where(place_ref[:, k:k + 1] == at, weight_ref[:, k:k + 1], 0.0)
+            mix_ref[:, c * 128:(c + 1) * 128] = part.astype(jnp.bfloat16)
+        for copy in loads(come[u], slot):
+            copy.wait()
+        if u + 1 < n_units:
+            fetch(come[u + 1], 1 - slot)
+        x2 = x_ref.at[slot].reshape(rows, 2 * half)
+
+        def mix_step(n, carry):
+            total_ref[:, block_at(n)] += dot32(mix_ref[...], x2[:, block_at(n)])
+            return carry
+
+        lax.fori_loop(0, 2 * half // WIDE, mix_step, 0)
+
+    fetch(come[0], 0)
+    for u in units:
+        mix(u, u % 2)
+    sum_ref[...] = total_ref[...].astype(jnp.bfloat16)
+    for u in units:
         for phase in range(3):
             go[u].wait_send(phase)
             come[u].wait_send(phase)
 
 
-def moe_exchange(rows, gate_pair, up_pair, down_pair):
+def moe_exchange(rows, normed, hidden, place, weight, gate_pair, up_pair, down_pair, sgate_pair, sup_pair, sdown_pair):
     n_units, width = rows.shape[0], rows.shape[-1]
+    n_tokens = normed.shape[0]
     anywhere = pl.BlockSpec(memory_space=pl.ANY)
+    vmem = pl.BlockSpec(memory_space=pltpu.VMEM)
     weights = (*gate_pair, *up_pair, *down_pair)
+    shared = (*sgate_pair, *sup_pair, *sdown_pair)
     inner = gate_pair[0].shape[1]
 
     def blocks(*lead):
         return jax.ShapeDtypeStruct((n_units, *lead, BLOCK, width), jnp.bfloat16)
 
     cube = (RING, RING, RING, BLOCK, width)
-    outs = (blocks(4, 4, 4), blocks(4, 4, 3), blocks(4, 3, 4), blocks(3, 4, 4), blocks(4, 4, 4), blocks(4, 4, 3), blocks(4, 3, 4))
+    steps = [blocks(4, 4, 3), blocks(4, 3, 4), blocks(3, 4, 4)]
+    outs = [jax.ShapeDtypeStruct((n_tokens, width), jnp.bfloat16)] + steps + [blocks(4, 4, 4)] + steps
     sems = pltpu.SemaphoreType.DMA
     return pl.pallas_call(
-        functools.partial(moe_kernel, n_units),
-        out_shape=outs,
-        in_specs=[anywhere] * 7,
-        out_specs=(anywhere,) * 7,
+        functools.partial(moe_kernel, n_units, place.shape[1]),
+        out_shape=tuple(outs),
+        in_specs=[anywhere] + [vmem] * 4 + [anywhere] * 12,
+        out_specs=(vmem,) + (anywhere,) * 7,
         scratch_shapes=[pltpu.VMEM(w.shape, jnp.bfloat16) for w in weights] + [
+            pltpu.VMEM((2, 4, width // 2, WIDE), jnp.bfloat16),
+            pltpu.VMEM((2, 2, WIDE, width // 2), jnp.bfloat16),
             pltpu.VMEM((2, *cube), jnp.bfloat16),
             pltpu.VMEM((RING ** 3 * BLOCK, inner), jnp.bfloat16),
             pltpu.VMEM((2, *cube), jnp.bfloat16),
-            sems((6,)), sems((2, 4)), sems((2,)), sems((2, 3)),
+            pltpu.VMEM((n_tokens, width), jnp.float32),
+            pltpu.VMEM((n_tokens, RING ** 3 * BLOCK), jnp.bfloat16),
+            sems((6,)), sems((2, 6)), sems((2, 4)), sems((2,)),
             sems((n_units, 3)), sems((n_units, 3)), sems((n_units, 3)), sems((n_units, 3)),
         ],
-        compiler_params=pltpu.CompilerParams(collective_id=0, has_side_effects=True, vmem_limit_bytes=48 * 1024 * 1024),
+        compiler_params=pltpu.CompilerParams(collective_id=0, has_side_effects=True, vmem_limit_bytes=60 * 1024 * 1024),
         cost_estimate=pl.CostEstimate(flops=250_000_000_000, bytes_accessed=100_000_000, transcendentals=0),
         name="moe_exchange",
-    )(rows, *weights)[0]
+    )(rows, normed, hidden, place, weight, *weights, *shared)[0]
 
 
 def solution(mesh):
@@ -307,19 +361,13 @@
         row_iota = jnp.arange(n_rows, dtype=jnp.int32)
         gates = gate_vals.reshape(n_tokens, top_k)
         picks = sum((row_iota[:, None] == row_of[None, :, k]).astype(jnp.bfloat16) for k in range(top_k))
-        spread = sum(jnp.where(row_of[:, k, None] == row_iota[None, :], gates[:, k, None], jnp.bfloat16(0)) for k in range(top_k))
 
         hidden = attention_block(x_in, qkv_pair, out_pair, fs)
         normed = rms_norm(hidden)
         buffer = dot32(picks, normed).astype(jnp.bfloat16)
         rows = buffer.reshape(capacity // BLOCK, RING, RING, RING, BLOCK, model_dim)
 
-        halves = split_cols(normed, fs)
-        shared_act = (jax.nn.silu(paired_dot(halves, sgate_pair)) * paired_dot(halves, sup_pair)).astype(jnp.bfloat16)
-        base = hidden.astype(jnp.float32) + join_cols(shared_act, sdown_pair, fs)
-
-        returned = moe_exchange(rows, gate_pair, up_pair, down_pair).reshape(n_rows, model_dim)
-        summed = base + dot32(spread, returned)
-        return summed.astype(jnp.bfloat16).reshape(n_batch, seq_len, model_dim)
+        summed = moe_exchange(rows, normed, hidden, row_of, gates.astype(jnp.float32), gate_pair, up_pair, down_pair, sgate_pair, sup_pair, sdown_pair)
+        return summed.reshape(n_batch, seq_len, model_dim)
 
     return jax.shard_map(local_step, mesh=mesh, in_specs=(tok_spec, row_spec, row_spec, P("ep", "fsdp", None), P("ep", "fsdp", None), P("ep", None, "fsdp"), row_spec, row_spec, P(None, "fsdp"), tok_spec, tok_spec, tok_spec), out_specs=tok_spec, check_vma=False)

time: 447 us -> 410 us (0.917)
  matrix products: 91 us -> 43.7 us
  Pallas kernels: 318 us -> 325 us
  local copies, waits for them, and re-layouts: 10.7 us -> 17.4 us
    dot_general x12 -> x5, matrix products: 81.2 us -> 36.7 us  [dot32(): return jnp.dot(left, right, preferred_element_type=jnp.float32)]
    pallas_call x1, Pallas kernels: 318 us -> 325 us  [moe_exchange(): pl.pallas_call(functools.partial(moe_kernel, n_units, place.shape[1]), ou...]
    unnamed x72 -> x32, local copies, waits for them, and re-layouts: 7.12 us -> 13.7 us
  transfers between devices with their start and end apart: 8 -> 8, of which waited for: 1 -> 1; matrix products, arithmetic and copies ran while one was open for 23% -> 17% of each run, Pallas kernels for 0% -> 0%
where the time goes in v3:
time: 410 us; the launch traced here: 405 us
  Pallas kernels  325 us (79%)
  matrix products  43.7 us (11%)
  local copies, waits for them, and re-layouts  17.4 us (4%)
  other arithmetic  13.6 us (3%)
    pallas_call x1, Pallas kernels, moe_exchange(): pl.pallas_call(functools.partial(moe_kernel, n_units, place.shape[1]), ou...  325 us
    dot_general x5, matrix products, dot32(): return jnp.dot(left, right, preferred_element_type=jnp.float32)  36.7 us
    unnamed x32, local copies, waits for them, and re-layouts  13.7 us
  transfers between devices with their start and end apart: 8, of which 1 were waited for; matrix products, arithmetic and copies ran while one was open for 17% of the time, Pallas kernels for 0%

profile of v3, /device:TPU:0, one launch (start us, length us, event | category | flops | bytes accessed | tf_op | source)
XLA Modules:
  0.0 404.7 jit_solution(914229811271671354)
XLA Ops:
  0.0 0.5 collective-permute-start.2
  0.5 0.5 collective-permute-start.5
  1.0 0.9 copy.26
  1.9 0.8 copy.21
  2.7 0.8 copy.20
  3.6 0.7 iota_compare_fusion.6
  4.3 0.8 fusion.69.place_ref
  5.1 1.2 slice_reduce_fusion.5
  6.3 0.4 fusion.16
  6.7 0.7 bitcast_convert_fusion.weight_ref
  7.4 0.7 fusion.74
  8.5 8.0 %fusion.52 = f32[384,6144]{1,0:T(8,128)S(1)} fusion(bf16[1024,6144]{1,0:T(8,128)(2,1)} %param.13, bf16[1,384,2048]{2,1,0:T(8,128)(2,1)S(1)} %fusion.17, s32[]{:T(128)S(6)} %select_n.68), kind=kOutput, calls=%fused_computation.68 | convolution fusion | flops 4831838208 | bytes 22806532 | tf_op jit(solution)/shard_map/dot_general | solution.py:41
  16.6 2.5 collective-permute-done
  19.1 0.3 collective-permute-start.7
  19.5 10.3 %fusion.35 = bf16[48,8,48,128]{3,1,2,0:T(8,128)(2,1)S(1)} fusion(f32[384,6144]{1,0:T(8,128)S(1)} %fusion.52, bf16[1024,6144]{1,0:T(8,128)(2,1)} %collective-permute-done, bf16[1,384,2048]{2,1,0:T(8,128)(2,1)S(1)} %fusion.17, s32[]{:T(128)S(6)} %select_n.69), kind=kOutput, calls=%fused_computation.49 | convolution fusion | flops 4836556800 | bytes 27525124 | tf_op jit(solution)/shard_map/dot_general | solution.py:41
  29.7 1.3 copy.31
  31.0 2.5 fusion.84
  33.5 2.9 copy.28
  36.3 2.2 fusion.48
  38.5 2.3 fusion.39
  40.9 1.9 fusion.41
  42.8 5.1 %fusion.85 = (f32[16,384]{1,0:T(8,128)S(1)}, f32[16,384,384]{1,2,0:T(8,128)}) fusion(f32[16,384,384]{1,2,0:T(8,128)S(1)} %fusion.41, pred[384,384]{0,1:T(8,128)(4,1)S(1)} %copy-done.6), kind=kOutput, calls=%fused_computation.139 | output fusion | flops 14156159 | bytes 19046400 | tf_op jit(solution)/shard_map/sub | solution.py:66
  47.9 5.1 %fusion.36 = bf16[16,128,384]{2,1,0:T(8,128)(2,1)S(1)} fusion(f32[16,384,384]{1,2,0:T(8,128)} %get-tuple-element.25, f32[16,384]{1,0:T(8,128)S(1)} %get-tuple-element.24, bf16[1,384,1,16,128]{1,4,3,2,0:T(8,128)(2,1)S(1)} %copy-done.4), kind=kOutput, calls=%fused_computation.50 | convolution fusion | flops 609484800 | bytes 12607488 | tf_op jit(solution)/shard_map/bhqk,bkhd->bqhd/dot_general | solution.py:67
  53.1 0.4 collective-permute-start.3
  53.7 0.8 copy-done.1
  54.5 1.9 fusion.55
  56.4 4.5 %fusion.12 = (f32[384]{0:T(512)S(1)}, bf16[384,2048]{1,0:T(8,128)(2,1)S(1)}) fusion(f32[384,2048]{1,0:T(8,128)S(1)} %fusion.55, bf16[1024,2048]{1,0:T(8,128)(2,1)} %collective-permute-done.1, bf16[384,2048]{0,1:T(8,128)(2,1)S(1)} %bitcast.105, s32[]{:T(128)S(6)} %select_n.69, bf16[1,384,2048]{2,1,0:T(8,128)(2,1)S(1)} %copy-done), kind=kOutput, calls=%fused_computation.28 | convolution fusion | flops 1616117376 | bytes 11273732 | tf_op jit(solution)/shard_map/dot_general | solution.py:41
  61.6 12.1 %convolution_convert_fusion = bf16[3072,2048]{1,0:T(8,128)(2,1)} fusion(bf16[384,2048]{1,0:T(8,128)(2,1)S(1)} %fusion.13.normed_ref, s32[384]{0:T(512)S(1)} %get-tuple-element.8, s32[384]{0:T(512)S(1)} %get-tuple-element.9, s32[384]{0:T(512)S(1)} %get-tuple-element.10, s32[384]{0:T(512)S(1)} %copy-done.7, s32[384]{0:T(512)S(1)} %copy-done.8, ...), kind=kOutput, calls=%fused_computation.1 | convolution fusion | flops 4866441216 | bytes 14164992 | tf_op jit(solution)/shard_map/dot_general | solution.py:41
  73.7 1.5 copy-done.11
  75.2 1.6 copy-done.12
  76.8 324.9 %moe_exchange.1 = (bf16[384,2048]{1,0:T(8,128)(2,1)}, bf16[6,4,4,3,8,2048]{5,4,3,2,1,0:T(8,128)(2,1)}, bf16[6,4,3,4,8,2048]{5,4,3,2,1,0:T(8,128)(2,1)}, bf16[6,3...) custom-call(bf16[6,4,4,4,8,2048]{5,4,3,2,1,0:T(8,128)(2,1)} %bitcast, ...), custom_call_target="tpu_custom_call" | custom-call | flops 249999998976 | bytes 100000000 | tf_op jit(solution)/shard_map/moe_exchange/pallas_call | solution.py:307
  401.7 2.7 copy.39
  (39 shorter events, 1.2 us)
Async XLA Ops:
  0.0 6.3 %copy-start = (bf16[1,384,2048]{2,1,0:T(8,128)(2,1)S(1)}, bf16[1,384,2048]{2,1,0:T(8,128)(2,1)}, u32[]{:S(2)}) copy-start(bf16[1,384,2048]{2,1,0:T(8,128)(2,1)} %param.12) | copy-start | bytes 4718596
  0.0 19.1 %collective-permute-start = (bf16[1024,6144]{1,0:T(8,128)(2,1)}, bf16[1024,6144]{1,0:T(8,128)(2,1)}, u32[]{:S(2)}, u32[]{:S(2)}) collective-permute-start(bf16[1024,6144]{1,0:T(8,128)(2,1)} %param.13), channel_id=1, source_target_pairs={{0,64},{64,0},{1,65},{65,1},{2,66},{66,2},{3,67},{67,3},{4,68},{68... | collective-permute-start | bytes 37748744 | tf_op jit(solution)/shard_map/ppermute | solution.py:344
  0.0 53.1 %collective-permute-start.2 = (bf16[1024,1408]{1,0:T(8,128)(2,1)}, bf16[1024,1408]{1,0:T(8,128)(2,1)}, u32[]{:S(2)}, u32[]{:S(2)}) collective-permute-start(bf16[1024,1408]{1,0:T(8,128)(2,1)} %bitcast.107), channel_id=1, source_target_pairs={{0,64},{64,0},{1,65},{65,1},{2,66},{66,2},{3,67},{67,3},{4,68},{68... | collective-permute-start | bytes 8650760 | tf_op jit(solution)/shard_map/ppermute | solution.py:344
  0.5 53.0 %collective-permute-start.1 = (bf16[1024,2048]{1,0:T(8,128)(2,1)}, bf16[1024,2048]{1,0:T(8,128)(2,1)}, u32[]{:S(2)}, u32[]{:S(2)}) collective-permute-start(bf16[1024,2048]{1,0:T(8,128)(2,1)} %param.14), channel_id=1, source_target_pairs={{0,64},{64,0},{1,65},{65,1},{2,66},{66,2},{3,67},{67,3},{4,68},{68... | collective-permute-start | bytes 12582920 | tf_op jit(solution)/shard_map/ppermute | solution.py:344
  0.5 74.7 %collective-permute-start.5 = (bf16[1024,2816]{1,0:T(8,128)(2,1)}, bf16[1024,2816]{1,0:T(8,128)(2,1)}, u32[]{:S(2)}, u32[]{:S(2)}) collective-permute-start(bf16[1024,2816]{1,0:T(8,128)(2,1)} %sgate_a.1), channel_id=1, source_target_pairs={{0,64},{64,0},{1,65},{65,1},{2,66},{66,2},{3,67},{67,3},{4,68},{68... | collective-permute-start | bytes 17301512 | tf_op jit(solution)/shard_map/ppermute | solution.py:344
  1.0 75.8 %collective-permute-start.6 = (bf16[1024,2816]{1,0:T(8,128)(2,1)}, bf16[1024,2816]{1,0:T(8,128)(2,1)}, u32[]{:S(2)}, u32[]{:S(2)}) collective-permute-start(bf16[1024,2816]{1,0:T(8,128)(2,1)} %sup_a.1), channel_id=1, source_target_pairs={{0,64},{64,0},{1,65},{65,1},{2,66},{66,2},{3,67},{67,3},{4,68},{68... | collective-permute-start | bytes 17301512 | tf_op jit(solution)/shard_map/ppermute | solution.py:344
  5.1 3.4 copy-start.2
  19.1 57.7 %collective-permute-start.7 = (bf16[2816,1024]{1,0:T(8,128)(2,1)}, bf16[2816,1024]{1,0:T(8,128)(2,1)}, u32[]{:S(2)}, u32[]{:S(2)}) collective-permute-start(bf16[2816,1024]{1,0:T(8,128)(2,1)} %sdown_a.1), channel_id=1, source_target_pairs={{0,64},{64,0},{1,65},{65,1},{2,66},{66,2},{3,67},{67,3},{4,68},{68... | collective-permute-start | bytes 17301512 | tf_op jit(solution)/shard_map/ppermute | solution.py:344
  40.9 1.9 copy-start.6
  42.8 5.2 %copy-start.4 = (bf16[1,384,1,16,128]{1,4,3,2,0:T(8,128)(2,1)S(1)}, bf16[1,384,1,16,128]{1,4,3,2,0:T(8,128)(2,1)}, u32[]{:S(2)}) copy-start(bf16[1,384,1,16,128]{1,4,3,2,0:T(8,128)(2,1)} %copy.28) | copy-start | bytes 4718596
  47.9 5.2 %copy-start.9 = (bf16[1,1024,1408]{2,1,0:T(8,128)(2,1)S(1)}, bf16[1,1024,1408]{2,1,0:T(8,128)(2,1)}, u32[]{:S(2)}) copy-start(bf16[1,1024,1408]{2,1,0:T(8,128)(2,1)} %param.16) | copy-start | bytes 8650756
  47.9 5.6 %copy-start.10 = (bf16[1,1408,1024]{2,1,0:T(8,128)(2,1)S(1)}, bf16[1,1408,1024]{2,1,0:T(8,128)(2,1)}, u32[]{:S(2)}) copy-start(bf16[1,1408,1024]{2,1,0:T(8,128)(2,1)} %param.17) | copy-start | bytes 8650756
  47.9 6.6 %copy-start.1 = (bf16[1024,2048]{1,0:T(8,128)(2,1)S(1)}, bf16[1024,2048]{1,0:T(8,128)(2,1)}, u32[]{:S(2)}) copy-start(bf16[1024,2048]{1,0:T(8,128)(2,1)} %param.14) | copy-start | bytes 12582916
  53.1 20.6 %collective-permute-start.3 = (bf16[1024,1408]{1,0:T(8,128)(2,1)S(1)}, bf16[1024,1408]{1,0:T(8,128)(2,1)S(1)}, u32[]{:S(2)}, u32[]{:S(2)}) collective-permute-start(bf16[1024,1408]{1,0:T(8,128)(2,1)S(1)} %bitcast.110), channel_id=1, source_target_pairs={{0,64},{64,0},{1,65},{65,1},{2,66},{66,2},{3,67},{67,3},{4,68},{68... | collective-permute-start | bytes 8650760 | tf_op jit(solution)/shard_map/ppermute | solution.py:344
  53.5 20.2 %collective-permute-start.4 = (bf16[1408,1024]{1,0:T(8,128)(2,1)S(1)}, bf16[1408,1024]{1,0:T(8,128)(2,1)S(1)}, u32[]{:S(2)}, u32[]{:S(2)}) collective-permute-start(bf16[1408,1024]{1,0:T(8,128)(2,1)S(1)} %bitcast.112), channel_id=1, source_target_pairs={{0,64},{64,0},{1,65},{65,1},{2,66},{66,2},{3,67},{67,3},{4,68},{68... | collective-permute-start | bytes 8650760 | tf_op jit(solution)/shard_map/ppermute | solution.py:344
  60.9 12.8 %copy-start.3 = (bf16[384,2048]{1,0:T(8,128)(2,1)}, bf16[384,2048]{1,0:T(8,128)(2,1)S(1)}, u32[]{:S(2)}) copy-start(bf16[384,2048]{1,0:T(8,128)(2,1)S(1)} %get-tuple-element.27.hidden_ref) | copy-start | bytes 4718596
  60.9 0.7 copy-start.7
  60.9 0.7 copy-start.8
  61.3 12.4 %copy-start.5 = (bf16[384,2048]{1,0:T(8,128)(2,1)}, bf16[384,2048]{1,0:T(8,128)(2,1)S(1)}, u32[]{:S(2)}) copy-start(bf16[384,2048]{1,0:T(8,128)(2,1)S(1)} %fusion.13.normed_ref) | copy-start | bytes 4718596
  73.7 1.6 copy-start.11
  75.2 1.6 copy-start.12
